TPU v7x, 64 devices: a 2x2x8 block of a 4x4x8 slice. The times are simulated.
64 devices in a mesh: dp: 4 (over x, y), cp: 16 (over z, core).
Axes of the slice: x: 2, y: 2, z: 8, core: 2. Of those that a mesh axis runs over, the one named last changes fastest.
The devices are a block of a 4x4x8 slice.
Arguments:
- x_in: bfloat16 [12288, 8192], P(('dp', 'cp')), parts along dimension 0
- dy_in: bfloat16 [12288, 8192], P(('dp', 'cp')), parts along dimension 0
- doc_id: int32 [12288], P(('dp', 'cp')), parts along dimension 0
- w_q: bfloat16 [8192, 16, 128], replicated
- w_k: bfloat16 [8192, 2, 128], replicated
- w_v: bfloat16 [8192, 2, 128], replicated
- w_o: bfloat16 [16, 128, 8192], replicated
Outputs:
- output 1: bfloat16 [12288, 8192], P(('dp', 'cp')), parts along dimension 0
- output 2: bfloat16 [12288, 8192], P(('dp', 'cp')), parts along dimension 0
There are 4 independent parts. A program takes and returns all parts, laid end to end along the dimension named above; an argument that names none is the same for every part.
All inputs are finite; a program needn't handle non-finite values.
Results may differ from a plain program's by a relative error of at most 0.00987741.
Values are sent between devices in bfloat16 or wider.
A program may use at most 768 MiB of HBM per device.

v0:
```python
import jax
import jax.numpy as jnp
from jax import lax
from jax.sharding import PartitionSpec as P

NEG_BIG = -1.0e30


def stored_positions(seq_len, group_devs):
    tok_dev = seq_len // group_devs
    piece_len = tok_dev // 2
    row_idx = jnp.arange(seq_len, dtype=jnp.int32)
    owner_dev = row_idx // tok_dev
    offset = row_idx % tok_dev
    piece_idx = jnp.where(offset < piece_len, owner_dev, 2 * group_devs - 1 - owner_dev)
    return piece_idx * piece_len + offset % piece_len


def solution(mesh):
    group_devs = mesh.shape['cp']
    row_spec = P(('dp', 'cp'))
    full_spec = P()

    def local_layer(x_in, dy_in, doc_id, w_q, w_k, w_v, w_o):
        tok_dev, d_model = x_in.shape
        q_heads, head_dim = w_q.shape[1], w_q.shape[2]
        kv_heads = w_k.shape[1]
        q_group = q_heads // kv_heads
        seq_len = tok_dev * group_devs
        score_scale = head_dim ** -0.5
        wq_grp = w_q.reshape(d_model, kv_heads, q_group, head_dim)
        wo_grp = w_o.reshape(kv_heads, q_group, head_dim, d_model)
        all_pos = stored_positions(seq_len, group_devs)
        my_pos = lax.dynamic_slice_in_dim(all_pos, lax.axis_index('cp') * tok_dev, tok_dev)
        q_loc = jnp.einsum('td,dkge->tkge', x_in, wq_grp, preferred_element_type=jnp.float32).astype(jnp.bfloat16)
        k_loc = jnp.einsum('td,dke->tke', x_in, w_k, preferred_element_type=jnp.float32).astype(jnp.bfloat16)
        v_loc = jnp.einsum('td,dke->tke', x_in, w_v, preferred_element_type=jnp.float32).astype(jnp.bfloat16)
        k_all = lax.all_gather(k_loc, 'cp', axis=0, tiled=True)
        v_all = lax.all_gather(v_loc, 'cp', axis=0, tiled=True)
        doc_all = lax.all_gather(doc_id, 'cp', axis=0, tiled=True)
        visible = (all_pos[None, :] <= my_pos[:, None]) & (doc_all[None, :] == doc_id[:, None])
        scores = jnp.einsum('tkge,ske->tkgs', q_loc, k_all, preferred_element_type=jnp.float32) * score_scale
        scores = jnp.where(visible[:, None, None, :], scores, NEG_BIG)
        log_norm = jax.nn.logsumexp(scores, axis=-1, keepdims=True)
        prob_bf = jnp.exp(scores - log_norm).astype(jnp.bfloat16)
        out_loc = jnp.einsum('tkgs,ske->tkge', prob_bf, v_all, preferred_element_type=jnp.float32).astype(jnp.bfloat16)
        y_out = jnp.einsum('tkge,kged->td', out_loc, wo_grp, preferred_element_type=jnp.float32).astype(jnp.bfloat16)
        do_loc = jnp.einsum('td,kged->tkge', dy_in, wo_grp, preferred_element_type=jnp.float32).astype(jnp.bfloat16)
        delta_row = jnp.einsum('tkge,tkge->tkg', do_loc, out_loc, preferred_element_type=jnp.float32)
        d_prob = jnp.einsum('tkge,ske->tkgs', do_loc, v_all, preferred_element_type=jnp.float32)
        d_score = (prob_bf.astype(jnp.float32) * (d_prob - delta_row[:, :, :, None])).astype(jnp.bfloat16)
        dq_loc = (jnp.einsum('tkgs,ske->tkge', d_score, k_all, preferred_element_type=jnp.float32) * score_scale).astype(jnp.bfloat16)
        dk_part = jnp.einsum('tkgs,tkge->ske', d_score, q_loc, preferred_element_type=jnp.float32) * score_scale
        dv_part = jnp.einsum('tkgs,tkge->ske', prob_bf, do_loc, preferred_element_type=jnp.float32)
        dk_loc = lax.psum_scatter(dk_part, 'cp', scatter_dimension=0, tiled=True)
        dv_loc = lax.psum_scatter(dv_part, 'cp', scatter_dimension=0, tiled=True)
        dx_wide = (jnp.einsum('tkge,dkge->td', dq_loc, wq_grp, preferred_element_type=jnp.float32)
                   + jnp.einsum('tke,dke->td', dk_loc.astype(jnp.bfloat16), w_k, preferred_element_type=jnp.float32)
                   + jnp.einsum('tke,dke->td', dv_loc.astype(jnp.bfloat16), w_v, preferred_element_type=jnp.float32))
        return y_out, dx_wide.astype(jnp.bfloat16)

    return jax.shard_map(local_layer, mesh=mesh,
                         in_specs=(row_spec, row_spec, row_spec, full_spec, full_spec, full_spec, full_spec),
                         out_specs=(row_spec, row_spec), check_vma=False)
```

profile of v0, /device:TPU:21, one launch (start us, length us, event | category | flops | bytes accessed | tf_op | source)
XLA Modules:
  0.0 332.1 jit_solution(16346251099745527102)
XLA Ops:
  7.3 1.8 copy-done
  9.1 3.8 %fusion.73 = bf16[192,2,128]{2,0,1:T(8,128)(2,1)} fusion(bf16[8192,2,128]{2,1,0:T(2,128)(2,1)} %param.11, bf16[192,8192]{1,0:T(8,128)(2,1)S(1)} %copy-done), kind=kOutput, calls=%fused_computation.54 | convolution fusion | flops 805355520 | bytes 7438336 | tf_op jit(solution)/shard_map/td,dke->tke/dot_general | solution.py:36
  13.0 3.8 %fusion.68 = bf16[192,2,128]{2,0,1:T(8,128)(2,1)} fusion(bf16[8192,2,128]{2,1,0:T(2,128)(2,1)} %param.12, bf16[192,8192]{1,0:T(8,128)(2,1)S(1)} %copy-done), kind=kOutput, calls=%fused_computation.53 | convolution fusion | flops 805355520 | bytes 7438336 | tf_op jit(solution)/shard_map/td,dke->tke/dot_general | solution.py:37
  17.0 0.6 dynamic-slice
  18.3 0.3 dynamic-update-slice
  18.6 51.7 %all-reduce = s32[3072]{0:T(1024)S(1)} all-reduce(s32[3072]{0:T(1024)S(1)} %dynamic-update-slice), channel_id=1, replica_groups=mesh['dp'=4,'cp'=16] {'cp'}, use_global_device_ids=true, to_apply=%add | all-reduce | flops 3072 | bytes 24576
  70.2 17.8 %fusion.55 = bf16[192,2,8,128]{3,0,2,1:T(8,128)(2,1)} fusion(bf16[8192,2,8,128]{3,2,1,0:T(8,128)(2,1)} %bitcast.115, bf16[192,8192]{1,0:T(8,128)(2,1)S(1)} %copy-done), kind=kOutput, calls=%fused_computation.50 | convolution fusion | flops 6442844160 | bytes 37486592 | tf_op jit(solution)/shard_map/td,dkge->tkge/dot_general | solution.py:35
  88.0 0.1 dynamic_slice.3
  88.1 0.5 compare_and_fusion
  88.7 16.7 %fusion.8 = (f32[192,2,8]{0,2,1:T(8,128)S(1)}, f32[2,3072,192,8]{1,2,3,0:T(8,128)}) fusion(pred[192,3072]{1,0:T(8,128)(4,1)S(1)} %compare_and_fusion, bf16[192,2,8,128]{3,0,2,1:T(8,128)(2,1)} %fusion.55, bf16[3072,2,128]{2,0,1:T(8,128)(2,1)} %all-gather.5.cloned.1.call-done), kind=kOutput, calls=%fused_computation.12 | convolution fusion | flops 2444227584 | bytes 40710144 | tf_op jit(solution)/shard_map/tkge,ske->tkgs/dot_general | solution.py:42
  105.4 16.9 %exponential_reduce_fusion = f32[192,2,8]{0,2,1:T(8,128)S(1)} fusion(f32[2,3072,192,8]{1,2,3,0:T(8,128)} %get-tuple-element.3, f32[192,2,8]{0,2,1:T(8,128)S(1)} %is-finite_select_fusion, pred[192,3072]{1,0:T(8,128)(4,1)S(1)} %compare_and_fusion), kind=kLoop, calls=%fused_computation.5 | loop fusion | flops 37745664 | bytes 38363136 | tf_op jit(solution)/shard_map/reduce_sum | solution.py:44
  122.3 23.1 %exponential_convert_fusion = bf16[192,2,8,3072]{3,0,2,1:T(8,128)(2,1)} fusion(f32[2,3072,192,8]{1,2,3,0:T(8,128)} %get-tuple-element.3, f32[192,2,8]{0,2,1:T(8,128)S(1)} %log_add_fusion, pred[192,3072]{1,0:T(8,128)(4,1)S(1)} %compare_and_fusion), kind=kLoop, calls=%fused_computation.4 | loop fusion | flops 37748736 | bytes 57225216 | tf_op jit(solution)/shard_map/convert_element_type | solution.py:45
  145.3 9.6 %fusion.60 = bf16[192,2,8,128]{3,0,2,1:T(8,128)(2,1)S(1)} fusion(bf16[192,2,8,3072]{3,0,2,1:T(8,128)(2,1)} %exponential_convert_fusion, bf16[3072,2,128]{2,0,1:T(8,128)(2,1)} %all-gather.3.cloned.1.call-done), kind=kOutput, calls=%fused_computation.51 | convolution fusion | flops 2416312320 | bytes 21233664 | tf_op jit(solution)/shard_map/tkgs,ske->tkge/dot_general | solution.py:46
  155.0 17.6 %fusion.40 = (f32[192,2,8]{0,2,1:T(8,128)S(1)}, bf16[192,2,8,128]{3,0,2,1:T(8,128)(2,1)S(1)}) fusion(bf16[192,2,8,128]{3,0,2,1:T(8,128)(2,1)S(1)} %fusion.60, bf16[2,8,128,8192]{3,2,1,0:T(8,128)(2,1)} %bitcast.113, bf16[192,8192]{1,0:T(8,128)(2,1)} %param.8), kind=kOutput, calls=%fused_computation.42 | convolution fusion | flops 6444413952 | bytes 38285312 | tf_op jit(solution)/shard_map/td,kged->tkge/dot_general | solution.py:48
  172.6 16.3 %fusion.1 = bf16[192,2,8,3072]{3,0,2,1:T(8,128)(2,1)} fusion(bf16[192,2,8,3072]{3,0,2,1:T(8,128)(2,1)} %exponential_convert_fusion, f32[192,2,8]{0,2,1:T(8,128)S(1)} %get-tuple-element.4, bf16[192,2,8,128]{3,0,2,1:T(8,128)(2,1)S(1)} %get-tuple-element.5, bf16[3072,2,128]{2,0,1:T(8,128)(2,1)S(1)} %copy-done.3), kind=kOutput, calls=%fused_computation.2 | convolution fusion | flops 2453667840 | bytes 40120320 | tf_op jit(solution)/shard_map/tkge,ske->tkgs/dot_general | solution.py:50
  188.9 13.2 %fusion.26 = f32[3072,2,128]{2,0,1:T(8,128)} fusion(bf16[192,2,8,128]{3,0,2,1:T(8,128)(2,1)S(1)} %copy-done.2, bf16[192,2,8,3072]{3,0,2,1:T(8,128)(2,1)} %fusion.1), kind=kOutput, calls=%fused_computation.26 | convolution fusion | flops 2416705536 | bytes 22806528 | tf_op jit(solution)/shard_map/tkgs,tkge->ske/dot_general | solution.py:53
  202.2 13.3 %convolution_bitcast_fusion.2 = f32[3072,2,128]{2,0,1:T(8,128)} fusion(bf16[192,2,8,128]{3,0,2,1:T(8,128)(2,1)S(1)} %get-tuple-element.5, bf16[192,2,8,3072]{3,0,2,1:T(8,128)(2,1)} %exponential_convert_fusion), kind=kOutput, calls=%fused_computation.23 | convolution fusion | flops 2415919104 | bytes 22806528 | tf_op jit(solution)/shard_map/tkgs,tkge->ske/dot_general | solution.py:54
  215.6 10.3 %fusion.63 = bf16[192,2,8,128]{3,0,1,2:T(8,128)(2,1)} fusion(bf16[192,2,8,3072]{3,0,2,1:T(8,128)(2,1)} %fusion.1, bf16[3072,2,128]{2,0,1:T(8,128)(2,1)S(1)} %copy-done.4), kind=kOutput, calls=%fused_computation.52 | convolution fusion | flops 2416705536 | bytes 21233664 | tf_op jit(solution)/shard_map/tkgs,ske->tkge/dot_general | solution.py:52
  225.9 15.7 %fusion.22 = bf16[192,8192]{1,0:T(8,128)(2,1)} fusion(bf16[2,8,128,8192]{3,2,1,0:T(8,128)(2,1)} %bitcast.114, bf16[192,2,8,128]{3,0,2,1:T(8,128)(2,1)S(1)} %copy-done.6), kind=kOutput, calls=%fused_computation.22 | convolution fusion | flops 6444023808 | bytes 37486592 | tf_op jit(solution)/shard_map/tkge,kged->td/dot_general | solution.py:47
  241.6 17.1 %reduce-scatter.3.cloned.1.call-done = f32[192,2,128]{2,0,1:T(8,128)} async-done(((f32[3072,2,128]{2,0,1:T(8,128)}), f32[192,2,128]{2,0,1:T(8,128)}) %reduce-scatter.3.cloned.1.call-update) | async-done | bytes 196624 | tf_op jit(solution)/shard_map/reduce_scatter | solution.py:55
  258.7 6.5 %convolution_bitcast_fusion.1 = f32[192,8192]{1,0:T(8,128)} fusion(bf16[8192,2,128]{2,1,0:T(2,128)(2,1)} %param.11, f32[192,2,128]{2,0,1:T(8,128)} %reduce-scatter.3.cloned.1.call-done), kind=kOutput, calls=%fused_computation.18 | convolution fusion | flops 805355520 | bytes 10682368 | tf_op jit(solution)/shard_map/tke,dke->td/dot_general | solution.py:58
  265.2 32.4 %fusion.14 = f32[192,8192]{1,0:T(8,128)} fusion(f32[192,8192]{1,0:T(8,128)} %convolution_bitcast_fusion.1, bf16[192,2,8,128]{3,0,1,2:T(8,128)(2,1)} %fusion.63, bf16[8192,2,8,128]{3,2,1,0:T(8,128)(2,1)} %bitcast.116), kind=kOutput, calls=%fused_computation.16 | convolution fusion | flops 6444023808 | bytes 46923776 | tf_op jit(solution)/shard_map/tkge,dkge->td/dot_general | solution.py:57
  297.6 20.3 %reduce-scatter.5.cloned.1.call-done = f32[192,2,128]{2,0,1:T(8,128)} async-done(((f32[3072,2,128]{2,0,1:T(8,128)}), f32[192,2,128]{2,0,1:T(8,128)}) %reduce-scatter.5.cloned.1.call-update) | async-done | bytes 196624 | tf_op jit(solution)/shard_map/reduce_scatter | solution.py:56
  317.9 7.3 %fusion.21 = bf16[192,8192]{1,0:T(8,128)(2,1)} fusion(f32[192,8192]{1,0:T(8,128)} %fusion.14, bf16[8192,2,128]{2,1,0:T(2,128)(2,1)} %param.12, f32[192,2,128]{2,0,1:T(8,128)} %reduce-scatter.5.cloned.1.call-done), kind=kOutput, calls=%fused_computation.21 | convolution fusion | flops 808501248 | bytes 13828096 | tf_op jit(solution)/shard_map/tke,dke->td/dot_general | solution.py:59
  (31 shorter events, 0.6 us)
Async XLA Ops:
  7.2 1.9 copy-start
  7.2 81.5 %all-gather.5.cloned.1.call-start = ((), (), s32[]{:S(2)}) async-start(), calls=%async_computation.3 | async-start | bytes 1671168 | tf_op jit(solution)/shard_map/all_gather | solution.py:38
  12.9 4.1 %copy-start.8 = (u32[64]{0:T(128)S(1)}, u32[64]{0:T(128)}, u32[]{:S(2)}) copy-start(u32[64]{0:T(128)} %constant.52) | copy-start | bytes 772
  12.9 5.4 %copy-start.7 = (s32[192]{0:T(256)S(1)}, s32[192]{0:T(256)}, u32[]{:S(2)}) copy-start(s32[192]{0:T(256)} %param.9) | copy-start | bytes 2308
  13.0 132.4 %all-gather.3.cloned.1.call-start = ((), (), s32[]{:S(2)}) async-start(), calls=%async_computation.2 | async-start | bytes 1671168 | tf_op jit(solution)/shard_map/all_gather | solution.py:39
  16.9 241.8 %reduce-scatter.3.cloned.1.call-start = ((), (), s32[]{:S(2)}) async-start(), calls=%async_computation.4 | async-start | bytes 3342336 | tf_op jit(solution)/shard_map/reduce_scatter | solution.py:55
  155.0 17.6 %copy-start.5 = (bf16[192,2,8,128]{3,0,2,1:T(8,128)(2,1)}, bf16[192,2,8,128]{3,0,2,1:T(8,128)(2,1)S(1)}, u32[]{:S(2)}) copy-start(bf16[192,2,8,128]{3,0,2,1:T(8,128)(2,1)S(1)} %fusion.60) | copy-start | bytes 2359300
  155.0 17.6 %copy-start.3 = (bf16[3072,2,128]{2,0,1:T(8,128)(2,1)S(1)}, bf16[3072,2,128]{2,0,1:T(8,128)(2,1)}, u32[]{:S(2)}) copy-start(bf16[3072,2,128]{2,0,1:T(8,128)(2,1)} %all-gather.3.cloned.1.call-done) | copy-start | bytes 4718596
  172.6 16.3 %copy-start.2 = (bf16[192,2,8,128]{3,0,2,1:T(8,128)(2,1)S(1)}, bf16[192,2,8,128]{3,0,2,1:T(8,128)(2,1)}, u32[]{:S(2)}) copy-start(bf16[192,2,8,128]{3,0,2,1:T(8,128)(2,1)} %fusion.55) | copy-start | bytes 2359300
  202.1 13.5 %copy-start.4 = (bf16[3072,2,128]{2,0,1:T(8,128)(2,1)S(1)}, bf16[3072,2,128]{2,0,1:T(8,128)(2,1)}, u32[]{:S(2)}) copy-start(bf16[3072,2,128]{2,0,1:T(8,128)(2,1)} %all-gather.5.cloned.1.call-done) | copy-start | bytes 4718596
  202.2 115.8 %reduce-scatter.5.cloned.1.call-start = ((), (), s32[]{:S(2)}) async-start(), calls=%async_computation.5 | async-start | bytes 3342336 | tf_op jit(solution)/shard_map/reduce_scatter | solution.py:56
  215.6 10.3 %copy-start.6 = (bf16[192,2,8,128]{3,0,2,1:T(8,128)(2,1)S(1)}, bf16[192,2,8,128]{3,0,2,1:T(8,128)(2,1)}, u32[]{:S(2)}) copy-start(bf16[192,2,8,128]{3,0,2,1:T(8,128)(2,1)} %copy-done.5) | copy-start | bytes 2359300
  265.2 60.1 %copy-start.1 = (bf16[192,8192]{1,0:T(8,128)(2,1)S(1)}, bf16[192,8192]{1,0:T(8,128)(2,1)}, u32[]{:S(2)}) copy-start(bf16[192,8192]{1,0:T(8,128)(2,1)} %param.7) | copy-start | bytes 9437188
Sparse Core Ops, SparseCore 0:
  13.1 40.7 all-gather.4
  55.6 34.3 all-gather.2
  202.3 56.3 reduce-scatter.2
  260.9 56.9 reduce-scatter.4
where the time goes:
time: 338 us; the launch traced here: 332 us
  matrix products  184 us (54%)
  blocking collectives  51.7 us (15%)
  other arithmetic  40.5 us (12%)
  waiting for transfers between devices  37.6 us (11%)
  between operations  14.9 us (4%)
    unnamed x1, blocking collectives  51.7 us
    dot_general x1, matrix products, local_layer(): jnp.einsum('tkge,dkge->td', dq_loc, wq_grp, preferred_element_type=jnp.fl...  32.4 us
    convert_element_type x1, other arithmetic, local_layer(): prob_bf = jnp.exp(scores - log_norm).astype(jnp.bfloat16)  23.1 us
    reduce_scatter x1, waiting for transfers between devices, local_layer(): dv_loc = lax.psum_scatter(dv_part, 'cp', scatter_dimension=0, tiled=True)  20.3 us
    dot_general x1, matrix products, local_layer(): jnp.einsum('td,dkge->tkge', x_in, wq_grp, preferred_element_type=jnp.floa...  17.8 us
    dot_general x1, matrix products, local_layer(): jnp.einsum('td,kged->tkge', dy_in, wo_grp, preferred_element_type=jnp.flo...  17.6 us
    reduce_scatter x1, waiting for transfers between devices, local_layer(): dk_loc = lax.psum_scatter(dk_part, 'cp', scatter_dimension=0, tiled=True)  17.1 us
    reduce_sum x1, other arithmetic, local_layer(): log_norm = jax.nn.logsumexp(scores, axis=-1, keepdims=True)  16.9 us
  transfers between devices with their start and end apart: 4, of which 2 were waited for; matrix products, arithmetic and copies ran while one was open for 48% of the time, Pallas kernels for 0%

commit v1 on v0

v1 whole, which is shorter than its diff:
```python
import functools

import jax
import jax.numpy as jnp
from jax import lax
from jax.experimental import pallas as pl
from jax.experimental.pallas import tpu as pltpu
from jax.sharding import PartitionSpec as P

MESH = pl.DeviceIdType.MESH
NEG_BIG = -1.0e30
LOG2E = 1.4426950408889634
F32, BF16 = jnp.float32, jnp.bfloat16
NT = (((1,), (1,)), ((), ()))
NN = (((1,), (0,)), ((), ()))
DOC_VALUES = 9


def dot(a, b, dims=NN):
    return lax.dot_general(a, b, dims, preferred_element_type=F32)


def remote(src, dst, send, recv, dev):
    return pltpu.make_async_remote_copy(src_ref=src, dst_ref=dst, send_sem=send, recv_sem=recv,
                                        device_id={'cp': dev}, device_id_type=MESH)


def ring_ids(chips):
    me = lax.axis_index('cp')
    core, chip = lax.rem(me, 2), me // 2
    return core, chip, chip * 2 + 1 - core, lax.rem(chip + 1, chips) * 2 + core, lax.rem(chip + chips - 1, chips) * 2 + core


def entry_barrier(devs):
    barrier = pltpu.get_barrier_semaphore()
    for dev in devs:
        pl.semaphore_signal(barrier, inc=1, device_id={'cp': dev}, device_id_type=MESH)
    pl.semaphore_wait(barrier, len(devs))


def proj_kernel(chips, x, dy, meta, wq, wk, wv, wo, q_o, do_o, kv_o, md_o,
                xb, dyb, mb, kvb, wkb, wvb, wqb, wob, scr, wr, wkv, acc, kvacc,
                loc, wksem, wqsem, wosem, xs, xr, ys, yr, ms, mr, gs, gr, osem):
    half = x.shape[0] // 2
    d_model = x.shape[1]
    tok = 2 * half
    pieces = 2 * chips
    n_ch = xs.shape[1]
    cw = d_model // n_ch
    core, chip, partner, up, down = ring_ids(chips)
    row_off = (pl.multiple_of(half * core, half), pl.multiple_of(3 * half - half * core, half))
    n_q, qd = d_model // wqb.shape[1], wqb.shape[1]
    group = wqb.shape[2]
    head = wqb.shape[3]
    n_o = group * head // wob.shape[1]

    def wq_copy(i, slot):
        return pltpu.make_async_copy(wq.at[pl.ds(i * qd, qd), core], wqb.at[slot], wqsem.at[slot])

    def wo_copy(i, slot):
        rows = wob.shape[1]
        return pltpu.make_async_copy(wo.at[pl.ds(core * group * head + i * rows, rows)], wob.at[slot], wosem.at[slot])

    wk_copies = []
    for ch in range(n_ch):
        rows = pl.ds(ch * 2 * cw, 2 * cw)
        wk_copies.append((pltpu.make_async_copy(wk.at[rows], wkb.at[rows], wksem.at[0, ch]),
                          pltpu.make_async_copy(wv.at[rows], wvb.at[rows], wksem.at[1, ch])))
    x_loc, y_loc, x_rem, y_rem = [], [], [], []
    for ch in range(n_ch):
        cols = pl.ds(ch * cw, cw)
        for pc in range(2):
            src = pl.ds(half * pc, half)
            dst = pl.ds(row_off[pc], half)
            x_loc.append(pltpu.make_async_copy(x.at[src, cols], xb.at[dst, cols], loc.at[0, pc, ch]))
            y_loc.append(pltpu.make_async_copy(dy.at[src, cols], dyb.at[dst, cols], loc.at[1, pc, ch]))
            x_rem.append(remote(x.at[src, cols], xb.at[dst, cols], xs.at[pc, ch], xr.at[pc, ch], partner))
            y_rem.append(remote(dy.at[src, cols], dyb.at[dst, cols], ys.at[pc, ch], yr.at[pc, ch], partner))
    m_loc = pltpu.make_async_copy(meta, mb.at[0], osem.at[0])
    m_rem = remote(meta, mb.at[1], ms, mr, partner)

    for ch in range(n_ch):
        x_loc[2 * ch].start()
        x_loc[2 * ch + 1].start()
        wk_copies[ch][0].start()
        wk_copies[ch][1].start()
    m_loc.start()
    for s in range(wqb.shape[0]):
        wq_copy(s, s).start()
    entry_barrier((partner, up, down))
    for c in x_rem:
        c.start()
    m_rem.start()
    for c in y_rem:
        c.start()
    for c in y_loc:
        c.start()
    for s in range(wob.shape[0]):
        wo_copy(s, s).start()

    for ch in range(n_ch):
        for c in (x_loc[2 * ch], x_loc[2 * ch + 1]):
            c.wait()
        for c in wk_copies[ch]:
            c.wait()
        for part, buf in ((0, wkb), (1, wvb)):
            base = part * 2 * cw
            scr[base:base + 2 * cw, :] = buf[ch * 2 * cw:(ch + 1) * 2 * cw, :].astype(F32)
            wkv[:, part * head:(part + 1) * head] = scr[pl.ds(base + core, cw, stride=2), :].astype(BF16)
        for c in (x_rem[2 * ch], x_rem[2 * ch + 1]):
            c.wait_recv()
        part_sum = dot(xb[:, ch * cw:(ch + 1) * cw], wkv[...])
        if ch == 0:
            kvacc[...] = part_sum
        else:
            kvacc[...] += part_sum
    m_loc.wait()
    m_rem.wait_recv()
    lo, hi = chip, pieces - 1 - chip
    width = md_o.shape[2]
    for pc, idx in ((0, lo), (1, hi)):
        both = (mb[0, pc].astype(F32) + mb[1, pc].astype(F32)).astype(BF16)
        md_o[pc] = both[:, :width]
        kvb[idx, 2 * tok:2 * tok + 16] = both[:, width:]
        kvb[idx, 0:tok] = kvacc[pc * tok:(pc + 1) * tok, 0:head].astype(BF16)
        kvb[idx, tok:2 * tok] = kvacc[pc * tok:(pc + 1) * tok, head:].astype(BF16)

    last = chips // 2 - 1

    def hop(direction, t, pc):
        src = lax.rem(chip + (chips - t if direction == 0 else t), chips)
        idx = src if pc == 0 else pieces - 1 - src
        return remote(kvb.at[idx], kvb.at[idx], gs.at[direction, t, pc], gr.at[direction, t, pc], up if direction == 0 else down)

    def arrived(direction, t, pc):
        src = lax.rem(chip + (chips - t - 1 if direction == 0 else t + 1), chips)
        idx = src if pc == 0 else pieces - 1 - src
        remote(kvb.at[idx], kvb.at[idx], gs.at[direction, t, pc], gr.at[direction, t, pc], up).wait_recv()

    moves = [[(d, pc) for pc in range(2) for d in range(2) if t < last or d == pc] for t in range(last + 1)]

    def advance(t):
        for d, pc in moves[t - 1]:
            arrived(d, t - 1, pc)
            if t <= last and (d, pc) in moves[t]:
                hop(d, t, pc).start()

    for d, pc in moves[0]:
        hop(d, 0, pc).start()

    acc[...] = jnp.zeros_like(acc)
    sub = 128
    n_slot = wqb.shape[0]

    @pl.loop(0, n_q)
    def _(i):
        slot = lax.rem(i, n_slot)
        wq_copy(i, slot).wait()

        @pl.loop(0, qd // sub)
        def _(j):
            rows = pl.ds(pl.multiple_of(j * sub, sub), sub)
            scr[0:sub * group, :] = wqb[slot, rows].astype(F32).reshape(sub * group, head)
            for g in range(group):
                wr[rows, g * head:(g + 1) * head] = scr[pl.ds(g, sub, stride=group), :].astype(BF16)

        @pl.when(i + n_slot < n_q)
        def _():
            wq_copy(i + n_slot, slot).start()

        acc[...] += dot(xb[:, pl.ds(pl.multiple_of(i * qd, qd), qd)], wr[...])

        @pl.when(i == 4)
        def _():
            advance(1)

    for g in range(group):
        for pc in range(2):
            q_o[pc, g * tok:(g + 1) * tok, :] = acc[pc * tok:(pc + 1) * tok, g * head:(g + 1) * head].astype(BF16)
    advance(2)

    for c in y_loc:
        c.wait()
    for c in y_rem:
        c.wait_recv()

    wide = wob.shape[1] // head
    for i in range(n_o):
        slot = i % wob.shape[0]
        wo_copy(i, slot).wait()
        part = dot(dyb[...], wob[slot], NT).astype(BF16)
        for g in range(wide):
            for pc in range(2):
                do_o[pc, (i * wide + g) * tok:(i * wide + g + 1) * tok, :] = part[pc * tok:(pc + 1) * tok, g * head:(g + 1) * head]
        if i + wob.shape[0] < n_o:
            wo_copy(i + wob.shape[0], slot).start()
        if i == 1:
            advance(3)
    for t in range(4, last + 2):
        advance(t)
    out = pltpu.make_async_copy(kvb, kv_o, osem.at[0])
    out.start()
    for c in x_rem + y_rem + [m_rem]:
        c.wait_send()
    for t in range(last + 1):
        for d, pc in moves[t]:
            hop(d, t, pc).wait_send()
    out.wait()


def attn_kernel(chips, scale, q, do, kv, md, q_off, o_ref, dq_ref, dkv, s_scr, p_scr, ds_scr, acc_t, k_t, v_t, row_scr, m_ref, l_ref):
    pieces = 2 * chips
    tok = kv.shape[1] // 2 - 8
    head = kv.shape[2]
    lanes_all = q.shape[1]
    group = lanes_all // tok
    lw = 256
    n_lc = lanes_all // lw
    chip = lax.axis_index('cp') // 2
    dkv[...] = jnp.zeros_like(dkv)

    def prep(j, tot):
        v_t[j] = kv[j, tok:2 * tok].astype(F32).T.astype(BF16)
        k_t[j] = kv[j, 0:tok].astype(F32).T.astype(BF16)
        return tot + kv[j, 2 * tok:2 * tok + 16].astype(F32)

    tot = lax.fori_loop(0, pieces, prep, jnp.zeros((16, head), F32))[0:1]

    for pc in range(2):
        place = chip if pc == 0 else pieces - 1 - chip
        doc_q = md[pc].astype(F32)[0:1]
        start = jnp.zeros((1, lanes_all), F32)
        for v in range(1, DOC_VALUES):
            start = jnp.where(doc_q == float(v), tot[:, v:v + 1], start)
        first = jnp.min(start).astype(jnp.int32) // tok
        pos = q_off[...] + (place * tok).astype(F32)
        m_ref[...] = jnp.full_like(m_ref, NEG_BIG)
        l_ref[...] = jnp.zeros_like(l_ref)

        @pl.loop(first, place + 1)
        def _(kb):
            keys = kv[kb, 0:tok]
            u = (lax.broadcasted_iota(jnp.int32, (tok, lw), 0) + kb * tok).astype(F32)
            for lc in range(n_lc):
                ln = slice(lc * lw, (lc + 1) * lw)
                s = dot(keys, q[pc, ln], NT) * (scale * LOG2E)
                s = jnp.where((u >= start[:, ln]) & (u <= pos[:, ln]), s, NEG_BIG)
                s_scr[kb, :, ln] = s
                m_old = m_ref[:, ln]
                m_new = jnp.maximum(m_old, jnp.max(s, axis=0, keepdims=True))
                l_ref[:, ln] = l_ref[:, ln] * jnp.exp2(m_old - m_new) + jnp.sum(jnp.exp2(s - m_new), axis=0, keepdims=True)
                m_ref[:, ln] = m_new

        log_norm = m_ref[...] + jnp.log2(l_ref[...])
        acc_t[...] = jnp.zeros_like(acc_t)

        @pl.loop(first, place + 1)
        def _(kb):
            for lc in range(n_lc):
                ln = slice(lc * lw, (lc + 1) * lw)
                p = jnp.exp2(s_scr[kb, :, ln] - log_norm[:, ln]).astype(BF16)
                p_scr[kb, :, ln] = p
                acc_t[:, ln] += dot(v_t[kb], p)

        for lc in range(n_lc):
            ln = slice(lc * lw, (lc + 1) * lw)
            o_bf = acc_t[:, ln].astype(BF16).astype(F32)
            do_t = do[pc, ln].astype(F32).T
            l_ref[:, ln] = jnp.sum(do_t * o_bf, axis=0, keepdims=True)
            row_scr[ln, :] = o_bf.T.astype(BF16)
        for g in range(group):
            o_ref[pc * tok:(pc + 1) * tok, g * head:(g + 1) * head] = row_scr[g * tok:(g + 1) * tok, :]
        acc_t[...] = jnp.zeros_like(acc_t)

        @pl.loop(first, place + 1)
        def _(kb):
            vals = kv[kb, tok:2 * tok]
            for lc in range(n_lc):
                ln = slice(lc * lw, (lc + 1) * lw)
                dp = dot(vals, do[pc, ln], NT)
                ds = (p_scr[kb, :, ln].astype(F32) * (dp - l_ref[:, ln])).astype(BF16)
                ds_scr[:, ln] = ds
                acc_t[:, ln] += dot(k_t[kb], ds)
            dkv[kb, tok:2 * tok] += dot(p_scr[kb], do[pc])
            dkv[kb, 0:tok] += dot(ds_scr[...], q[pc]) * scale

        for lc in range(n_lc):
            ln = slice(lc * lw, (lc + 1) * lw)
            row_scr[ln, :] = (acc_t[:, ln] * scale).T.astype(BF16)
        for g in range(group):
            dq_ref[pc * tok:(pc + 1) * tok, g * head:(g + 1) * head] = row_scr[g * tok:(g + 1) * tok, :]


def out_kernel(chips, o, dq, dkv, wo, wq, wk, wv, y, dx,
               ob, dqb, own, ring, fin, a2, b2, wob, wqb, wkb, scr, wr, dacc, yb, xo,
               loc, ex_s, ex_r, rs, rr, fs, fr, wosem, wqsem, wksem, ysem, xsem, ys, yr, xs, xr):
    tok = own.shape[1] // 2
    head = own.shape[2]
    half = tok // 2
    pieces = 2 * chips
    d_half = yb.shape[1]
    core, chip, partner, up, down = ring_ids(chips)
    mine = (pl.multiple_of(half * core, half), pl.multiple_of(3 * half - half * core, half))
    theirs = (pl.multiple_of(half - half * core, half), pl.multiple_of(2 * half + half * core, half))
    hw = o.shape[1]
    col0 = pl.multiple_of(core * d_half, d_half)
    bw = wob.shape[2]
    n_y = d_half // bw
    qd = wqb.shape[1] * head // wr.shape[1]
    n_x = d_half // qd
    n_head = wr.shape[1] // head
    kc = scr.shape[0] // 2

    def wo_copy(i, slot):
        return pltpu.make_async_copy(wo.at[:, pl.ds(pl.multiple_of(col0 + i * bw, bw), bw)], wob.at[slot], wosem.at[slot])

    def wq_copy(i, slot):
        rows = wqb.shape[1]
        return pltpu.make_async_copy(wq.at[pl.ds(pl.multiple_of(col0 * n_head + i * rows, rows), rows)], wqb.at[slot], wqsem.at[slot])

    rows = pl.ds(pl.multiple_of(col0 * 2, 2 * d_half), 2 * d_half)
    wk_copies = [pltpu.make_async_copy(w.at[rows], wkb.at[k], wksem.at[k]) for k, w in enumerate((wk, wv))]
    ocols = pl.ds(pl.multiple_of(core * hw, hw), hw)
    l_own = pltpu.make_async_copy(dkv, own, loc.at[0])
    l_o = pltpu.make_async_copy(o, ob.at[:, ocols], loc.at[1])
    l_dq = pltpu.make_async_copy(dq, dqb.at[:, ocols], loc.at[2])
    r_o = remote(o, ob.at[:, ocols], ex_s.at[0], ex_r.at[0], partner)
    r_dq = remote(dq, dqb.at[:, ocols], ex_s.at[1], ex_r.at[1], partner)

    l_own.start()
    l_o.start()
    l_dq.start()
    for s in range(wob.shape[0]):
        wo_copy(s, s).start()
    entry_barrier((partner, up, down))
    r_o.start()
    r_dq.start()
    for s in range(wqb.shape[0]):
        wq_copy(s, s).start()
    for c in wk_copies:
        c.start()

    steps = chips - 1

    def owner(direction, s):
        chip_w = lax.rem(chip + (2 * chips - 1 - s if direction == 0 else 1 + s), chips)
        return chip_w if direction == 0 else pieces - 1 - chip_w

    def part_rows(kvp):
        return pl.ds(kvp * tok, tok)

    def send(direction, s, kvp):
        src = own.at[owner(direction, 0), part_rows(kvp)] if s == 0 else ring.at[direction, s - 1, kvp]
        return remote(src, ring.at[direction, s, kvp], rs.at[direction, s, kvp], rr.at[direction, s, kvp], up if direction == 0 else down)

    def advance(s):
        for kvp in range(2):
            for d in range(2):
                remote(ring.at[d, s - 1, kvp], ring.at[d, s - 1, kvp], rs.at[d, s - 1, kvp], rr.at[d, s - 1, kvp], up).wait_recv()
                if s <= steps - 1:
                    ring[d, s - 1, kvp] = ring[d, s - 1, kvp] + own[owner(d, s), part_rows(kvp)]
                    send(d, s, kvp).start()
                else:
                    total = ring[d, s - 1, kvp] + own[owner(d, s), part_rows(kvp)]
                    fin[d * tok:(d + 1) * tok, kvp * head:(kvp + 1) * head] = total.astype(BF16)

    l_own.wait()
    for kvp in range(2):
        for d in range(2):
            send(d, 0, kvp).start()

    def out_copies(buf, dst, i, width, lsem, ssem, rsem):
        cols = pl.ds(pl.multiple_of(col0 + i * width, width), width)
        bc = pl.ds(pl.multiple_of(i * width, width), width)
        for pc in range(2):
            pltpu.make_async_copy(buf.at[pl.ds(mine[pc], half), bc], dst.at[pl.ds(half * pc, half), cols], lsem).start()
            remote(buf.at[pl.ds(theirs[pc], half), bc], dst.at[pl.ds(half * pc, half), cols], ssem, rsem, partner).start()

    l_o.wait()
    r_o.wait_recv()
    ns = wob.shape[0]

    @pl.loop(0, n_y)
    def _(i):
        slot = lax.rem(i, ns)
        wo_copy(i, slot).wait()
        yb[:, pl.ds(pl.multiple_of(i * bw, bw), bw)] = dot(ob[...], wob[slot]).astype(BF16)

        @pl.when(i + ns < n_y)
        def _():
            wo_copy(i + ns, slot).start()

        @pl.when(i > 0)
        def _():
            out_copies(yb, y, i - 1, bw, ysem, ys, yr)

        @pl.when(i == 4)
        def _():
            advance(1)

    out_copies(yb, y, n_y - 1, bw, ysem, ys, yr)
    advance(2)

    l_dq.wait()
    r_dq.wait_recv()
    nq = wqb.shape[0]
    sub = 64

    @pl.loop(0, n_x)
    def _(i):
        slot = lax.rem(i, nq)
        wq_copy(i, slot).wait()

        @pl.loop(0, qd // sub)
        def _(j):
            src = pl.ds(pl.multiple_of(j * sub * n_head, sub * n_head), sub * n_head)
            dst = pl.ds(pl.multiple_of(j * sub, sub), sub)
            scr[0:sub * n_head, :] = wqb[slot, src].astype(F32)
            for g in range(n_head):
                wr[dst, g * head:(g + 1) * head] = scr[pl.ds(g, sub, stride=n_head), :].astype(BF16)

        @pl.when(i + nq < n_x)
        def _():
            wq_copy(i + nq, slot).start()

        dacc[:, pl.ds(pl.multiple_of(i * qd, qd), qd)] = dot(dqb[...], wr[...], NT)

        @pl.when(i == 3)
        def _():
            advance(3)

    advance(4)
    for c in wk_copies:
        c.wait()
    for k in range(2):
        for j in range(d_half // kc):
            scr[...] = wkb[k, j * 2 * kc:(j + 1) * 2 * kc].astype(F32)
            for h in range(2):
                b2[j * kc:(j + 1) * kc, (2 * k + h) * head:(2 * k + h + 1) * head] = scr[pl.ds(h, kc, stride=2), :].astype(BF16)
    for s in range(5, steps + 1):
        advance(s)

    r_fin = remote(fin, a2.at[core], fs, fr, partner)
    r_fin.start()
    a2[core] = fin[...]
    r_fin.wait_recv()
    a_all = jnp.concatenate([a2[0][:, :head], a2[1][:, :head], a2[0][:, head:], a2[1][:, head:]], axis=1)
    for i in range(n_y):
        cs = slice(i * bw, (i + 1) * bw)
        xo[:, cs] = (dacc[:, cs] + dot(a_all, b2[cs, :], NT)).astype(BF16)
        if i > 0:
            out_copies(xo, dx, i - 1, bw, xsem, xs, xr)
    out_copies(xo, dx, n_y - 1, bw, xsem, xs, xr)

    for c in (r_o, r_dq, r_fin):
        c.wait_send()
    for s in range(steps):
        for kvp in range(2):
            for d in range(2):
                send(d, s, kvp).wait_send()
    for buf, dst, lsem, ssem, rsem in ((yb, y, ysem, ys, yr), (xo, dx, xsem, xs, xr)):
        cols = pl.ds(col0, d_half)
        pltpu.make_async_copy(buf.at[pl.ds(0, tok)], dst.at[:, cols], lsem).wait()
        both = remote(buf.at[pl.ds(0, tok)], dst.at[:, cols], ssem, rsem, partner)
        both.wait_send()
        both.wait_recv()


def solution(mesh):
    group_devs = mesh.shape['cp']
    chips = group_devs // 2
    row_spec = P(('dp', 'cp'))
    full_spec = P()
    any_spec = pl.BlockSpec(memory_space=pl.ANY)
    vmem_spec = pl.BlockSpec(memory_space=pltpu.VMEM)
    dma = pltpu.SemaphoreType.DMA

    def local_layer(x_in, dy_in, doc_id, w_q, w_k, w_v, w_o):
        tok, d_model = x_in.shape
        q_heads, head = w_q.shape[1], w_q.shape[2]
        kv_heads = w_k.shape[1]
        group = q_heads // kv_heads
        half = tok // 2
        rows2 = 2 * tok
        pieces = 2 * chips
        lanes = group * tok
        d_half = d_model // 2
        scale = head ** -0.5
        core = lax.axis_index('cp') % 2
        docs = doc_id.reshape(2, half)
        slot = jnp.stack([core, 1 - core])[:, None]
        lane = jnp.arange(tok)
        docf = jnp.concatenate([docs, docs], axis=1).astype(F32)
        docf = jnp.where((lane // half)[None, :] == slot, docf, 0.0)
        ids = jnp.tile(docf, (1, group))
        counts = jnp.sum((docs[:, :, None] < jnp.arange(head)[None, None, :]).astype(F32), axis=1)
        meta = jnp.concatenate([ids, counts], axis=1).astype(BF16)
        meta = jnp.broadcast_to(meta[:, None, :], (2, 16, lanes + head))
        q_off = jnp.tile(lane.astype(F32), (group,))[None, :]

        wq4 = w_q.reshape(d_model, kv_heads, group, head)
        wq2 = w_q.reshape(d_model * q_heads, head)
        wk2 = w_k.reshape(d_model * kv_heads, head)
        wv2 = w_v.reshape(d_model * kv_heads, head)
        wo2 = w_o.reshape(q_heads * head, d_model)

        n_ch = 4
        cw = d_model // n_ch
        qd = d_model // 8
        hops = chips // 2
        kv_rows = 2 * tok + 16
        q, do, kv, md = pl.pallas_call(
            functools.partial(proj_kernel, chips),
            name='proj',
            out_shape=(jax.ShapeDtypeStruct((2, lanes, head), BF16), jax.ShapeDtypeStruct((2, lanes, head), BF16),
                       jax.ShapeDtypeStruct((pieces, kv_rows, head), BF16), jax.ShapeDtypeStruct((2, 16, lanes), BF16)),
            in_specs=[any_spec] * 7,
            out_specs=(vmem_spec, vmem_spec, any_spec, vmem_spec),
            scratch_shapes=[
                pltpu.VMEM((rows2, d_model), BF16), pltpu.VMEM((rows2, d_model), BF16), pltpu.VMEM((2, 2, 16, lanes + head), BF16),
                pltpu.VMEM((pieces, kv_rows, head), BF16),
                pltpu.VMEM((2 * d_model, head), BF16), pltpu.VMEM((2 * d_model, head), BF16),
                pltpu.VMEM((3, qd, group, head), BF16), pltpu.VMEM((2, 2 * head, d_model), BF16),
                pltpu.VMEM((4 * cw, head), F32), pltpu.VMEM((qd, group * head), BF16), pltpu.VMEM((cw, 2 * head), BF16),
                pltpu.VMEM((rows2, group * head), F32), pltpu.VMEM((rows2, 2 * head), F32),
                dma((2, 2, n_ch)), dma((2, n_ch)), dma((3,)), dma((2,)),
                dma((2, n_ch)), dma((2, n_ch)), dma((2, n_ch)), dma((2, n_ch)), dma, dma,
                dma((2, hops, 2)), dma((2, hops, 2)), dma((1,)),
            ],
            compiler_params=pltpu.CompilerParams(collective_id=0, has_side_effects=True, vmem_limit_bytes=60 << 20),
        )(x_in, dy_in, meta, wq4, wk2, wv2, wo2)

        o, dq, dkv = pl.pallas_call(
            functools.partial(attn_kernel, chips, scale),
            name='attn',
            out_shape=(jax.ShapeDtypeStruct((rows2, group * head), BF16), jax.ShapeDtypeStruct((rows2, group * head), BF16),
                       jax.ShapeDtypeStruct((pieces, 2 * tok, head), F32)),
            in_specs=[vmem_spec] * 5,
            out_specs=(vmem_spec,) * 3,
            scratch_shapes=[
                pltpu.VMEM((pieces, tok, lanes), F32), pltpu.VMEM((pieces, tok, lanes), BF16), pltpu.VMEM((tok, lanes), BF16),
                pltpu.VMEM((head, lanes), F32), pltpu.VMEM((pieces, head, tok), BF16), pltpu.VMEM((pieces, head, tok), BF16),
                pltpu.VMEM((lanes, head), BF16), pltpu.VMEM((1, lanes), F32), pltpu.VMEM((1, lanes), F32),
            ],
            compiler_params=pltpu.CompilerParams(vmem_limit_bytes=60 << 20),
        )(q, do, kv, md, q_off)

        steps = chips - 1
        bw = d_half // 8
        y, dx = pl.pallas_call(
            functools.partial(out_kernel, chips),
            name='out',
            out_shape=(jax.ShapeDtypeStruct((tok, d_model), BF16), jax.ShapeDtypeStruct((tok, d_model), BF16)),
            in_specs=[any_spec] * 7,
            out_specs=(any_spec, any_spec),
            scratch_shapes=[
                pltpu.VMEM((rows2, q_heads * head), BF16), pltpu.VMEM((rows2, q_heads * head), BF16),
                pltpu.VMEM((pieces, 2 * tok, head), F32), pltpu.VMEM((2, steps, 2, tok, head), F32),
                pltpu.VMEM((rows2, 2 * head), BF16), pltpu.VMEM((2, rows2, 2 * head), BF16), pltpu.VMEM((d_half, 4 * head), BF16),
                pltpu.VMEM((3, q_heads * head, bw), BF16), pltpu.VMEM((3, bw * q_heads, head), BF16),
                pltpu.VMEM((2, 2 * d_half, head), BF16),
                pltpu.VMEM((2 * d_half // 4, head), F32), pltpu.VMEM((bw, q_heads * head), BF16),
                pltpu.VMEM((rows2, d_half), F32), pltpu.VMEM((rows2, d_half), BF16), pltpu.VMEM((rows2, d_half), BF16),
                dma((3,)), dma((2,)), dma((2,)), dma((2, steps, 2)), dma((2, steps, 2)), dma, dma,
                dma((3,)), dma((3,)), dma((2,)), dma, dma, dma, dma, dma, dma,
            ],
            compiler_params=pltpu.CompilerParams(collective_id=1, has_side_effects=True, vmem_limit_bytes=62 << 20),
        )(o, dq, dkv, wo2, wq2, wk2, wv2)
        return y, dx

    return jax.shard_map(local_layer, mesh=mesh,
                         in_specs=(row_spec, row_spec, row_spec, full_spec, full_spec, full_spec, full_spec),
                         out_specs=(row_spec, row_spec), check_vma=False)
```

time: 338 us -> 151 us (0.45); the launches traced: 332 us -> 149 us
  matrix products: 184 us -> 0 us
  Pallas kernels: 0 us -> 140 us
  blocking collectives: 51.7 us -> 0 us
  other arithmetic: 40.5 us -> 0.28 us
  waiting for transfers between devices: 37.6 us -> 0 us
  between operations: 14.9 us -> 0.69 us
  local copies, waits for them, and re-layouts: 2.81 us -> 7.86 us
    dot_general x14 -> x0, matrix products: 184 us -> none  [the longest x1 32.4 us: local_layer(): jnp.einsum('tkge,dkge->td', dq_loc, wq_grp, preferred_element_type=jnp.fl...]
    pallas_call x0 -> x3, Pallas kernels: none -> 140 us  [the longest x1 69.8 us: local_layer(): pl.pallas_call(functools.partial(out_kernel, chips), name='out', out_shap...]
    unnamed x1 -> x0, blocking collectives: 51.7 us -> none
    reduce_scatter x2 -> x0, waiting for transfers between devices: 37.4 us -> none  [the longest x1 20.3 us: local_layer(): dv_loc = lax.psum_scatter(dv_part, 'cp', scatter_dimension=0, tiled=True)]
    convert_element_type x1, other arithmetic: 23.1 us -> 0.01 us  [local_layer(): q_off = jnp.tile(lane.astype(F32), (group,))[None, :]]
    reduce_sum x1, other arithmetic: 16.9 us -> 0.11 us  [local_layer(): jnp.sum((docs[:, :, None] < jnp.arange(head)[None, None, :]).astype(F32),...]
  transfers between devices with their start and end apart: 4 -> 0, of which waited for: 2 -> 0; matrix products, arithmetic and copies ran while one was open for 48% -> 0% of each run, Pallas kernels for 0% -> 0%
where the time goes in v1:
time: 151 us; the launch traced here: 149 us
  Pallas kernels  140 us (93%)
  local copies, waits for them, and re-layouts  7.86 us (5%)
    pallas_call x1, Pallas kernels, local_layer(): pl.pallas_call(functools.partial(out_kernel, chips), name='out', out_shap...  69.8 us
    pallas_call x1, Pallas kernels, local_layer(): pl.pallas_call(functools.partial(proj_kernel, chips), name='proj', out_sh...  49.9 us
    pallas_call x1, Pallas kernels, local_layer(): pl.pallas_call(functools.partial(attn_kernel, chips, scale), name='attn',...  20.2 us
    unnamed x4, local copies, waits for them, and re-layouts  5.68 us

profile of v1, /device:TPU:21, one launch (start us, length us, event | category | flops | bytes accessed | tf_op | source)
XLA Modules:
  0.0 148.7 jit_solution(1221443851056551729)
XLA Ops:
  0.6 0.1 pad_add_fusion
  0.7 0.8 concatenate.19
  1.5 0.1 convert_reduce_fusion
  1.6 0.1 fusion
  1.7 0.1 concatenate.21
  1.8 0.7 broadcast_in_dim_tile.3.q_off
  2.5 0.7 broadcast_in_dim.7.meta
  3.1 49.9 %proj.1 = (bf16[2,1536,128]{2,1,0:T(8,128)(2,1)}, bf16[2,1536,128]{2,1,0:T(8,128)(2,1)}, bf16[16,400,128]{2,1,0:T(8,128)(2,1)}, bf16[2,16,1536]{2,1,0:T(8,128)(2,1)}) custom-call(bf16[192,8192]{1,0:T(8,128)(2,1)} %x.1, bf16[192,8192]{1,0:T(8,128)(2,1)} %dy.1, bf16[2,16,1664]{2,1,0:T(8,128)(2,1)} %broadcast_in_dim.7.meta, bf16[8192,2,8,128]{3,2,1,0:T(8,128)(2,1)} %bitcast.7, ...), custom_call_target="tpu_custom_call" | custom-call | tf_op jit(solution)/shard_map/proj/pallas_call | solution.py:512
  53.0 20.2 %attn.1 = (bf16[384,1024]{1,0:T(8,128)(2,1)}, bf16[384,1024]{1,0:T(8,128)(2,1)}, f32[16,384,128]{2,1,0:T(8,128)}) custom-call(bf16[2,1536,128]{2,1,0:T(8,128)(2,1)} %get-tuple-element.9.q, bf16[2,1536,128]{2,1,0:T(8,128)(2,1)} %get-tuple-element.10.do, bf16[16,400,128]{2,1,0:T(8,128)(2,1)} %get-tuple-element.11.kv, ...), custom_call_target="tpu_custom_call" | custom-call | tf_op jit(solution)/shard_map/attn/pallas_call | solution.py:533
  73.2 69.8 %out.1 = (bf16[192,8192]{1,0:T(8,128)(2,1)}, bf16[192,8192]{1,0:T(8,128)(2,1)}) custom-call(bf16[384,1024]{1,0:T(8,128)(2,1)} %get-tuple-element.13.o, bf16[384,1024]{1,0:T(8,128)(2,1)} %get-tuple-element.14.dq, f32[16,384,128]{2,1,0:T(8,128)} %get-tuple-element.15.dkv, bf16[2048,8192]{1,0:T(8,128)(2,1)} %bitcast.10, bf16[131072,128]{1,0:T(8,128)(2,1)} %bitcast.8, ...), custom_call_target="tpu_custom_call" | custom-call | tf_op jit(solution)/shard_map/out/pallas_call | solution.py:550
  143.0 0.0 copy-start
  143.0 4.0 %copy.11 = bf16[192,8192]{1,0:T(8,128)(2,1)} copy(bf16[192,8192]{1,0:T(8,128)(2,1)} %get-tuple-element.18) | data formatting | bytes 6291456
  147.1 0.0 copy-done
  147.1 1.7 %copy.12 = bf16[192,8192]{1,0:T(8,128)(2,1)} copy(bf16[192,8192]{1,0:T(8,128)(2,1)S(1)} %copy-done) | data formatting | bytes 6291456
  (5 shorter events, 0.0 us)
Async XLA Ops:
  143.0 4.0 %copy-start = (bf16[192,8192]{1,0:T(8,128)(2,1)S(1)}, bf16[192,8192]{1,0:T(8,128)(2,1)}, u32[]{:S(2)}) copy-start(bf16[192,8192]{1,0:T(8,128)(2,1)} %get-tuple-element.19) | copy-start | bytes 9437188

commit v2 on v1

--- a/solution.py
+++ b/solution.py
@@ -38,8 +38,31 @@
     pl.semaphore_wait(barrier, len(devs))
 
 
+TILE = 256
+PER = 8
+
+
+def sort_matrix():
+    toks = TILE // PER
+    r = lax.broadcasted_iota(jnp.int32, (TILE, TILE), 0)
+    c = lax.broadcasted_iota(jnp.int32, (TILE, TILE), 1)
+    t = r & (toks - 1)
+    return jnp.where(c == t * PER + lax.shift_right_logical(r, toks.bit_length() - 1), 1.0, 0.0).astype(BF16)
+
+
+def split_heads(order, src, dst, count, n_head, head):
+    toks = TILE // PER
+    for h0 in range(0, n_head, PER):
+        for t0 in range(0, count, 4 * toks):
+            side = [src[t0 + k * toks:t0 + (k + 1) * toks, h0:h0 + PER, :].reshape(TILE, head) for k in range(4)]
+            rows = dot(order, jnp.concatenate(side, axis=1)).astype(BF16)
+            for k in range(4):
+                for g in range(PER):
+                    dst[t0 + k * toks:t0 + (k + 1) * toks, (h0 + g) * head:(h0 + g + 1) * head] = rows[g * toks:(g + 1) * toks, k * head:(k + 1) * head]
+
+
 def proj_kernel(chips, x, dy, meta, wq, wk, wv, wo, q_o, do_o, kv_o, md_o,
-                xb, dyb, mb, kvb, wkb, wvb, wqb, wob, scr, wr, wkv, acc, kvacc,
+                xb, dyb, mb, kvb, wkb, wvb, wqb, wob, wr, order, pick, wkv, acc, kvacc,
                 loc, wksem, wqsem, wosem, xs, xr, ys, yr, ms, mr, gs, gr, osem):
     half = x.shape[0] // 2
     d_model = x.shape[1]
@@ -58,8 +81,9 @@
         return pltpu.make_async_copy(wq.at[pl.ds(i * qd, qd), core], wqb.at[slot], wqsem.at[slot])
 
     def wo_copy(i, slot):
-        rows = wob.shape[1]
-        return pltpu.make_async_copy(wo.at[pl.ds(core * group * head + i * rows, rows)], wob.at[slot], wosem.at[slot])
+        rows, kw = wob.shape[1], wob.shape[2]
+        n, k = i // (d_model // kw), i % (d_model // kw)
+        return pltpu.make_async_copy(wo.at[pl.ds(core * group * head + n * rows, rows), pl.ds(k * kw, kw)], wob.at[slot], wosem.at[slot])
 
     wk_copies = []
     for ch in range(n_ch):
@@ -98,22 +122,40 @@
     for s in range(wob.shape[0]):
         wo_copy(s, s).start()
 
+    r = lax.broadcasted_iota(jnp.int32, pick.shape, 0)
+    pick[...] = jnp.where(lax.broadcasted_iota(jnp.int32, pick.shape, 1) == 2 * r + core, 1.0, 0.0).astype(BF16)
+    order[...] = sort_matrix()
+    n_sub = TILE // 2
+    for ch in range(n_ch):
+        for c in wk_copies[ch]:
+            c.wait()
+        for j in range(ch * cw // n_sub, (ch + 1) * cw // n_sub, 2):
+            side = [buf[t * 2 * n_sub:(t + 1) * 2 * n_sub, :] for t in (j, j + 1) for buf in (wkb, wvb)]
+            rows = dot(pick[...], jnp.concatenate(side, axis=1)).astype(BF16)
+            wkv[j * n_sub:(j + 1) * n_sub, :] = rows[:, :2 * head]
+            wkv[(j + 1) * n_sub:(j + 2) * n_sub, :] = rows[:, 2 * head:]
+    quarters = 2
+    qs = qd // quarters
+
+    def split_part(slot, dst, k):
+        split_heads(order[...], wqb.at[slot, k * qs:(k + 1) * qs], dst.at[k * qs:(k + 1) * qs], qs, group, head)
+
+    wq_copy(0, 0).wait()
+    for k in range(quarters):
+        split_part(0, wr.at[0], k)
+    wq_copy(wqb.shape[0], 0).start()
     for ch in range(n_ch):
         for c in (x_loc[2 * ch], x_loc[2 * ch + 1]):
             c.wait()
-        for c in wk_copies[ch]:
-            c.wait()
-        for part, buf in ((0, wkb), (1, wvb)):
-            base = part * 2 * cw
-            scr[base:base + 2 * cw, :] = buf[ch * 2 * cw:(ch + 1) * 2 * cw, :].astype(F32)
-            wkv[:, part * head:(part + 1) * head] = scr[pl.ds(base + core, cw, stride=2), :].astype(BF16)
         for c in (x_rem[2 * ch], x_rem[2 * ch + 1]):
             c.wait_recv()
-        part_sum = dot(xb[:, ch * cw:(ch + 1) * cw], wkv[...])
-        if ch == 0:
-            kvacc[...] = part_sum
-        else:
-            kvacc[...] += part_sum
+        hc = cw // 2
+        for k in range(2):
+            part_sum = dot(xb[:, ch * cw + k * hc:ch * cw + (k + 1) * hc], wkv[ch * cw + k * hc:ch * cw + (k + 1) * hc])
+            if ch == 0:
+                kvacc[k] = part_sum
+            else:
+                kvacc[k] += part_sum
     m_loc.wait()
     m_rem.wait_recv()
     lo, hi = chip, pieces - 1 - chip
@@ -122,8 +164,9 @@
         both = (mb[0, pc].astype(F32) + mb[1, pc].astype(F32)).astype(BF16)
         md_o[pc] = both[:, :width]
         kvb[idx, 2 * tok:2 * tok + 16] = both[:, width:]
-        kvb[idx, 0:tok] = kvacc[pc * tok:(pc + 1) * tok, 0:head].astype(BF16)
-        kvb[idx, tok:2 * tok] = kvacc[pc * tok:(pc + 1) * tok, head:].astype(BF16)
+        kv_sum = (kvacc[0, pc * tok:(pc + 1) * tok, :] + kvacc[1, pc * tok:(pc + 1) * tok, :]).astype(BF16)
+        kvb[idx, 0:tok] = kv_sum[:, 0:head]
+        kvb[idx, tok:2 * tok] = kv_sum[:, head:]
 
     last = chips // 2 - 1
 
@@ -139,45 +182,57 @@
 
     moves = [[(d, pc) for pc in range(2) for d in range(2) if t < last or d == pc] for t in range(last + 1)]
 
-    def advance(t):
+    def advance(t, only=None):
         for d, pc in moves[t - 1]:
-            arrived(d, t - 1, pc)
-            if t <= last and (d, pc) in moves[t]:
-                hop(d, t, pc).start()
+            if only is None or pc == only:
+                arrived(d, t - 1, pc)
+                if t <= last and (d, pc) in moves[t]:
+                    hop(d, t, pc).start()
 
     for d, pc in moves[0]:
         hop(d, 0, pc).start()
 
     acc[...] = jnp.zeros_like(acc)
-    sub = 128
     n_slot = wqb.shape[0]
-
-    @pl.loop(0, n_q)
-    def _(i):
-        slot = lax.rem(i, n_slot)
-        wq_copy(i, slot).wait()
-
-        @pl.loop(0, qd // sub)
-        def _(j):
-            rows = pl.ds(pl.multiple_of(j * sub, sub), sub)
-            scr[0:sub * group, :] = wqb[slot, rows].astype(F32).reshape(sub * group, head)
-            for g in range(group):
-                wr[rows, g * head:(g + 1) * head] = scr[pl.ds(g, sub, stride=group), :].astype(BF16)
-
-        @pl.when(i + n_slot < n_q)
-        def _():
-            wq_copy(i + n_slot, slot).start()
-
-        acc[...] += dot(xb[:, pl.ds(pl.multiple_of(i * qd, qd), qd)], wr[...])
-
-        @pl.when(i == 4)
-        def _():
-            advance(1)
+    nw = group * head // quarters
+
+    def q_step(i, cur, nxt):
+        slot = lax.rem(i + 1, n_slot)
+
+        @pl.when(i + 1 < n_q)
+        def _():
+            wq_copy(i + 1, slot).wait()
+
+        lhs = xb.at[:, pl.ds(pl.multiple_of(i * qd, qd), qd)]
+        for k in range(quarters):
+            cols = slice(k * nw, (k + 1) * nw)
+            acc[:, cols] += dot(lhs[...], cur[:, cols])
+            split_part(slot, nxt, k)
+
+        @pl.when(i + 1 + n_slot < n_q)
+        def _():
+            wq_copy(i + 1 + n_slot, slot).start()
+
+    @pl.loop(0, n_q // 2)
+    def _(h):
+        q_step(2 * h, wr.at[0], wr.at[1])
+        q_step(2 * h + 1, wr.at[1], wr.at[0])
+
+        @pl.when(h == 1)
+        def _():
+            advance(1, 0)
+
+        @pl.when(h == 2)
+        def _():
+            advance(1, 1)
+
+        @pl.when(h == 3)
+        def _():
+            advance(2, 0)
 
     for g in range(group):
         for pc in range(2):
             q_o[pc, g * tok:(g + 1) * tok, :] = acc[pc * tok:(pc + 1) * tok, g * head:(g + 1) * head].astype(BF16)
-    advance(2)
 
     for c in y_loc:
         c.wait()
@@ -185,17 +240,29 @@
         c.wait_recv()
 
     wide = wob.shape[1] // head
-    for i in range(n_o):
-        slot = i % wob.shape[0]
-        wo_copy(i, slot).wait()
-        part = dot(dyb[...], wob[slot], NT).astype(BF16)
-        for g in range(wide):
-            for pc in range(2):
-                do_o[pc, (i * wide + g) * tok:(i * wide + g + 1) * tok, :] = part[pc * tok:(pc + 1) * tok, g * head:(g + 1) * head]
-        if i + wob.shape[0] < n_o:
-            wo_copy(i + wob.shape[0], slot).start()
-        if i == 1:
-            advance(3)
+    kw = wob.shape[2]
+    n_k = d_model // kw
+    for u in range(n_o * n_k):
+        n, k = u // n_k, u % n_k
+        slot = u % wob.shape[0]
+        wo_copy(u, slot).wait()
+        part = dot(dyb[:, k * kw:(k + 1) * kw], wob[slot], NT)
+        if k == 0:
+            acc[:, 0:wide * head] = part
+        else:
+            acc[:, 0:wide * head] += part
+        if u + wob.shape[0] < n_o * n_k:
+            wo_copy(u + wob.shape[0], slot).start()
+        if k == n_k - 1:
+            for g in range(wide):
+                for pc in range(2):
+                    do_o[pc, (n * wide + g) * tok:(n * wide + g + 1) * tok, :] = acc[pc * tok:(pc + 1) * tok, g * head:(g + 1) * head].astype(BF16)
+        if u == 0:
+            advance(2, 1)
+        elif u == 1:
+            advance(3, 0)
+        elif u == 2:
+            advance(3, 1)
     for t in range(4, last + 2):
         advance(t)
     out = pltpu.make_async_copy(kvb, kv_o, osem.at[0])
@@ -261,6 +328,7 @@
                 p = jnp.exp2(s_scr[kb, :, ln] - log_norm[:, ln]).astype(BF16)
                 p_scr[kb, :, ln] = p
                 acc_t[:, ln] += dot(v_t[kb], p)
+            dkv[kb, tok:2 * tok] += dot(p_scr[kb], do[pc])
 
         for lc in range(n_lc):
             ln = slice(lc * lw, (lc + 1) * lw)
@@ -281,7 +349,6 @@
                 ds = (p_scr[kb, :, ln].astype(F32) * (dp - l_ref[:, ln])).astype(BF16)
                 ds_scr[:, ln] = ds
                 acc_t[:, ln] += dot(k_t[kb], ds)
-            dkv[kb, tok:2 * tok] += dot(p_scr[kb], do[pc])
             dkv[kb, 0:tok] += dot(ds_scr[...], q[pc]) * scale
 
         for lc in range(n_lc):
@@ -292,7 +359,7 @@
 
 
 def out_kernel(chips, o, dq, dkv, wo, wq, wk, wv, y, dx,
-               ob, dqb, own, ring, fin, a2, b2, wob, wqb, wkb, scr, wr, dacc, yb, xo,
+               ob, dqb, own, ring, fin, a2, b2, wob, wqb, wkb, scr, wr, order, dacc, yb, xo,
                loc, ex_s, ex_r, rs, rr, fs, fr, wosem, wqsem, wksem, ysem, xsem, ys, yr, xs, xr):
     tok = own.shape[1] // 2
     head = own.shape[2]
@@ -306,9 +373,9 @@
     col0 = pl.multiple_of(core * d_half, d_half)
     bw = wob.shape[2]
     n_y = d_half // bw
-    qd = wqb.shape[1] * head // wr.shape[1]
+    qd = wqb.shape[1]
     n_x = d_half // qd
-    n_head = wr.shape[1] // head
+    n_head = wqb.shape[2]
     kc = scr.shape[0] // 2
 
     def wo_copy(i, slot):
@@ -316,7 +383,7 @@
 
     def wq_copy(i, slot):
         rows = wqb.shape[1]
-        return pltpu.make_async_copy(wq.at[pl.ds(pl.multiple_of(col0 * n_head + i * rows, rows), rows)], wqb.at[slot], wqsem.at[slot])
+        return pltpu.make_async_copy(wq.at[pl.ds(pl.multiple_of(col0 + i * rows, rows), rows)], wqb.at[slot], wqsem.at[slot])
 
     rows = pl.ds(pl.multiple_of(col0 * 2, 2 * d_half), 2 * d_half)
     wk_copies = [pltpu.make_async_copy(w.at[rows], wkb.at[k], wksem.at[k]) for k, w in enumerate((wk, wv))]
@@ -346,23 +413,23 @@
         chip_w = lax.rem(chip + (2 * chips - 1 - s if direction == 0 else 1 + s), chips)
         return chip_w if direction == 0 else pieces - 1 - chip_w
 
-    def part_rows(kvp):
-        return pl.ds(kvp * tok, tok)
+    def part_rows(row):
+        return pl.ds(row, tok)
 
     def send(direction, s, kvp):
-        src = own.at[owner(direction, 0), part_rows(kvp)] if s == 0 else ring.at[direction, s - 1, kvp]
+        src = own.at[owner(direction, 0), part_rows(kvp * tok)] if s == 0 else ring.at[direction, s - 1, kvp]
         return remote(src, ring.at[direction, s, kvp], rs.at[direction, s, kvp], rr.at[direction, s, kvp], up if direction == 0 else down)
 
-    def advance(s):
-        for kvp in range(2):
+    def event(e):
+        s, kvp = e // 2 + 1, lax.rem(e, 2)
+        for d in range(2):
+            remote(ring.at[d, s - 1, kvp], ring.at[d, s - 1, kvp], rs.at[d, s - 1, kvp], rr.at[d, s - 1, kvp], up).wait_recv()
+            ring[d, s - 1, kvp] = ring[d, s - 1, kvp] + own[owner(d, s), part_rows(pl.multiple_of(kvp * tok, tok))]
+
+        @pl.when(s < steps)
+        def _():
             for d in range(2):
-                remote(ring.at[d, s - 1, kvp], ring.at[d, s - 1, kvp], rs.at[d, s - 1, kvp], rr.at[d, s - 1, kvp], up).wait_recv()
-                if s <= steps - 1:
-                    ring[d, s - 1, kvp] = ring[d, s - 1, kvp] + own[owner(d, s), part_rows(kvp)]
-                    send(d, s, kvp).start()
-                else:
-                    total = ring[d, s - 1, kvp] + own[owner(d, s), part_rows(kvp)]
-                    fin[d * tok:(d + 1) * tok, kvp * head:(kvp + 1) * head] = total.astype(BF16)
+                remote(ring.at[d, s - 1, kvp], ring.at[d, s, kvp], rs.at[d, s, kvp], rr.at[d, s, kvp], up if d == 0 else down).start()
 
     l_own.wait()
     for kvp in range(2):
@@ -394,51 +461,72 @@
         def _():
             out_copies(yb, y, i - 1, bw, ysem, ys, yr)
 
-        @pl.when(i == 4)
-        def _():
-            advance(1)
+        @pl.when((i >= 3) & (lax.rem(i, 2) == 1))
+        def _():
+            event((i - 3) // 2)
 
     out_copies(yb, y, n_y - 1, bw, ysem, ys, yr)
-    advance(2)
 
     l_dq.wait()
     r_dq.wait_recv()
     nq = wqb.shape[0]
-    sub = 64
-
-    @pl.loop(0, n_x)
-    def _(i):
-        slot = lax.rem(i, nq)
-        wq_copy(i, slot).wait()
-
-        @pl.loop(0, qd // sub)
-        def _(j):
-            src = pl.ds(pl.multiple_of(j * sub * n_head, sub * n_head), sub * n_head)
-            dst = pl.ds(pl.multiple_of(j * sub, sub), sub)
-            scr[0:sub * n_head, :] = wqb[slot, src].astype(F32)
-            for g in range(n_head):
-                wr[dst, g * head:(g + 1) * head] = scr[pl.ds(g, sub, stride=n_head), :].astype(BF16)
-
-        @pl.when(i + nq < n_x)
-        def _():
-            wq_copy(i + nq, slot).start()
-
-        dacc[:, pl.ds(pl.multiple_of(i * qd, qd), qd)] = dot(dqb[...], wr[...], NT)
-
-        @pl.when(i == 3)
-        def _():
-            advance(3)
-
-    advance(4)
+    quarters = 2
+    qs = qd // quarters
+    order[...] = sort_matrix()
+
+    def split_part(slot, dst, k):
+        split_heads(order[...], wqb.at[slot, k * qs:(k + 1) * qs], dst.at[k * qs:(k + 1) * qs], qs, n_head, head)
+
+    wq_copy(0, 0).wait()
+    for k in range(quarters):
+        split_part(0, wr.at[0], k)
+    wq_copy(nq, 0).start()
+
+    def x_step(i, cur, nxt):
+        slot = lax.rem(i + 1, nq)
+
+        @pl.when(i + 1 < n_x)
+        def _():
+            wq_copy(i + 1, slot).wait()
+
+        dacc[:, pl.ds(pl.multiple_of(i * qd, qd), qd)] = dot(dqb[...], cur[...], NT)
+        for k in range(quarters):
+            split_part(slot, nxt, k)
+
+        @pl.when(i + 1 + nq < n_x)
+        def _():
+            wq_copy(i + 1 + nq, slot).start()
+
+    @pl.loop(0, n_x // 2)
+    def _(h):
+        x_step(2 * h, wr.at[0], wr.at[1])
+        event(3 + h)
+        x_step(2 * h + 1, wr.at[1], wr.at[0])
+
     for c in wk_copies:
         c.wait()
-    for k in range(2):
-        for j in range(d_half // kc):
-            scr[...] = wkb[k, j * 2 * kc:(j + 1) * 2 * kc].astype(F32)
-            for h in range(2):
-                b2[j * kc:(j + 1) * kc, (2 * k + h) * head:(2 * k + h + 1) * head] = scr[pl.ds(h, kc, stride=2), :].astype(BF16)
-    for s in range(5, steps + 1):
-        advance(s)
+    n_e = 2 * steps
+    first_e = 3 + n_x // 2
+
+    @pl.loop(first_e, n_e)
+    def _(e):
+        @pl.when(e < first_e + 4)
+        def _():
+            j = e - first_e
+            rows_b = d_half // 4
+            piece = kc // 2
+            for k in range(2):
+                for m in range(rows_b // piece):
+                    r0 = pl.multiple_of(j * rows_b + m * piece, piece)
+                    scr[k * kc:(k + 1) * kc, :] = wkb[k, pl.ds(2 * r0, kc), :].astype(F32)
+                    for h in range(2):
+                        b2[pl.ds(r0, piece), (2 * k + h) * head:(2 * k + h + 1) * head] = scr[pl.ds(k * kc + h, piece, stride=2), :].astype(BF16)
+
+        event(e)
+
+    for kvp in range(2):
+        for d in range(2):
+            fin[d * tok:(d + 1) * tok, kvp * head:(kvp + 1) * head] = ring[d, steps - 1, kvp].astype(BF16)
 
     r_fin = remote(fin, a2.at[core], fs, fr, partner)
     r_fin.start()
@@ -499,7 +587,6 @@
         q_off = jnp.tile(lane.astype(F32), (group,))[None, :]
 
         wq4 = w_q.reshape(d_model, kv_heads, group, head)
-        wq2 = w_q.reshape(d_model * q_heads, head)
         wk2 = w_k.reshape(d_model * kv_heads, head)
         wv2 = w_v.reshape(d_model * kv_heads, head)
         wo2 = w_o.reshape(q_heads * head, d_model)
@@ -520,9 +607,9 @@
                 pltpu.VMEM((rows2, d_model), BF16), pltpu.VMEM((rows2, d_model), BF16), pltpu.VMEM((2, 2, 16, lanes + head), BF16),
                 pltpu.VMEM((pieces, kv_rows, head), BF16),
                 pltpu.VMEM((2 * d_model, head), BF16), pltpu.VMEM((2 * d_model, head), BF16),
-                pltpu.VMEM((3, qd, group, head), BF16), pltpu.VMEM((2, 2 * head, d_model), BF16),
-                pltpu.VMEM((4 * cw, head), F32), pltpu.VMEM((qd, group * head), BF16), pltpu.VMEM((cw, 2 * head), BF16),
-                pltpu.VMEM((rows2, group * head), F32), pltpu.VMEM((rows2, 2 * head), F32),
+                pltpu.VMEM((3, qd, group, head), BF16), pltpu.VMEM((2, 4 * head, d_model // 2), BF16),
+                pltpu.VMEM((2, qd, group * head), BF16), pltpu.VMEM((TILE, TILE), BF16), pltpu.VMEM((TILE // 2, TILE), BF16), pltpu.VMEM((d_model, 2 * head), BF16),
+                pltpu.VMEM((rows2, group * head), F32), pltpu.VMEM((2, rows2, 2 * head), F32),
                 dma((2, 2, n_ch)), dma((2, n_ch)), dma((3,)), dma((2,)),
                 dma((2, n_ch)), dma((2, n_ch)), dma((2, n_ch)), dma((2, n_ch)), dma, dma,
                 dma((2, hops, 2)), dma((2, hops, 2)), dma((1,)),
@@ -557,15 +644,15 @@
                 pltpu.VMEM((rows2, q_heads * head), BF16), pltpu.VMEM((rows2, q_heads * head), BF16),
                 pltpu.VMEM((pieces, 2 * tok, head), F32), pltpu.VMEM((2, steps, 2, tok, head), F32),
                 pltpu.VMEM((rows2, 2 * head), BF16), pltpu.VMEM((2, rows2, 2 * head), BF16), pltpu.VMEM((d_half, 4 * head), BF16),
-                pltpu.VMEM((3, q_heads * head, bw), BF16), pltpu.VMEM((3, bw * q_heads, head), BF16),
+                pltpu.VMEM((3, q_heads * head, bw), BF16), pltpu.VMEM((3, bw, q_heads, head), BF16),
                 pltpu.VMEM((2, 2 * d_half, head), BF16),
-                pltpu.VMEM((2 * d_half // 4, head), F32), pltpu.VMEM((bw, q_heads * head), BF16),
+                pltpu.VMEM((1024, head), F32), pltpu.VMEM((2, bw, q_heads * head), BF16), pltpu.VMEM((TILE, TILE), BF16),
                 pltpu.VMEM((rows2, d_half), F32), pltpu.VMEM((rows2, d_half), BF16), pltpu.VMEM((rows2, d_half), BF16),
                 dma((3,)), dma((2,)), dma((2,)), dma((2, steps, 2)), dma((2, steps, 2)), dma, dma,
                 dma((3,)), dma((3,)), dma((2,)), dma, dma, dma, dma, dma, dma,
             ],
             compiler_params=pltpu.CompilerParams(collective_id=1, has_side_effects=True, vmem_limit_bytes=62 << 20),
-        )(o, dq, dkv, wo2, wq2, wk2, wv2)
+        )(o, dq, dkv, wo2, w_q, wk2, wv2)
         return y, dx
 
     return jax.shard_map(local_layer, mesh=mesh,

time: 151 us -> 136 us (0.901)
  the two profiles are of different devices: /device:TPU:21 before, /device:TPU:29 now
where the time goes in v2:
time: 136 us; the launch traced here: 138 us
  Pallas kernels  130 us (96%)
  local copies, waits for them, and re-layouts  7.86 us (6%)
    pallas_call x1, Pallas kernels, local_layer(): pl.pallas_call(functools.partial(out_kernel, chips), name='out', out_shap...  68.1 us
    pallas_call x1, Pallas kernels, local_layer(): pl.pallas_call(functools.partial(proj_kernel, chips), name='proj', out_sh...  41.2 us
    pallas_call x1, Pallas kernels, local_layer(): pl.pallas_call(functools.partial(attn_kernel, chips, scale), name='attn',...  20.3 us
    unnamed x4, local copies, waits for them, and re-layouts  5.68 us

profile of v2, /device:TPU:29, one launch (start us, length us, event | category | flops | bytes accessed | tf_op | source)
XLA Modules:
  0.0 138.4 jit_solution(16958200000248972266)
XLA Ops:
  0.6 0.1 pad_add_fusion
  0.7 0.8 concatenate.19
  1.5 0.1 convert_reduce_fusion
  1.6 0.1 fusion
  1.7 0.1 concatenate.21
  1.8 0.7 broadcast_in_dim_tile.3.q_off
  2.5 0.7 broadcast_in_dim.7.meta
  3.1 41.2 %proj.1 = (bf16[2,1536,128]{2,1,0:T(8,128)(2,1)}, bf16[2,1536,128]{2,1,0:T(8,128)(2,1)}, bf16[16,400,128]{2,1,0:T(8,128)(2,1)}, bf16[2,16,1536]{2,1,0:T(8,128)(2,1)}) custom-call(bf16[192,8192]{1,0:T(8,128)(2,1)} %x.1, bf16[192,8192]{1,0:T(8,128)(2,1)} %dy.1, bf16[2,16,1664]{2,1,0:T(8,128)(2,1)} %broadcast_in_dim.7.meta, bf16[8192,2,8,128]{3,2,1,0:T(8,128)(2,1)} %bitcast.6, ...), custom_call_target="tpu_custom_call" | custom-call | tf_op jit(solution)/shard_map/proj/pallas_call | solution.py:599
  44.3 20.3 %attn.1 = (bf16[384,1024]{1,0:T(8,128)(2,1)}, bf16[384,1024]{1,0:T(8,128)(2,1)}, f32[16,384,128]{2,1,0:T(8,128)}) custom-call(bf16[2,1536,128]{2,1,0:T(8,128)(2,1)} %get-tuple-element.9.q, bf16[2,1536,128]{2,1,0:T(8,128)(2,1)} %get-tuple-element.10.do, bf16[16,400,128]{2,1,0:T(8,128)(2,1)} %get-tuple-element.11.kv, ...), custom_call_target="tpu_custom_call" | custom-call | tf_op jit(solution)/shard_map/attn/pallas_call | solution.py:620
  64.6 68.1 %out.1 = (bf16[192,8192]{1,0:T(8,128)(2,1)}, bf16[192,8192]{1,0:T(8,128)(2,1)}) custom-call(bf16[384,1024]{1,0:T(8,128)(2,1)} %get-tuple-element.13.o, bf16[384,1024]{1,0:T(8,128)(2,1)} %get-tuple-element.14.dq, f32[16,384,128]{2,1,0:T(8,128)} %get-tuple-element.15.dkv, bf16[2048,8192]{1,0:T(8,128)(2,1)} %bitcast.8, bf16[8192,16,128]{2,1,0:T(8,128)(2,1)} %wq.1, ...), custom_call_target="tpu_custom_call" | custom-call | tf_op jit(solution)/shard_map/out/pallas_call | solution.py:637
  132.7 0.0 copy-start
  132.8 4.0 %copy.11 = bf16[192,8192]{1,0:T(8,128)(2,1)} copy(bf16[192,8192]{1,0:T(8,128)(2,1)} %get-tuple-element.18) | data formatting | bytes 6291456
  136.8 0.0 copy-done
  136.8 1.7 %copy.12 = bf16[192,8192]{1,0:T(8,128)(2,1)} copy(bf16[192,8192]{1,0:T(8,128)(2,1)S(1)} %copy-done) | data formatting | bytes 6291456
  (5 shorter events, 0.0 us)
Async XLA Ops:
  132.7 4.0 %copy-start = (bf16[192,8192]{1,0:T(8,128)(2,1)S(1)}, bf16[192,8192]{1,0:T(8,128)(2,1)}, u32[]{:S(2)}) copy-start(bf16[192,8192]{1,0:T(8,128)(2,1)} %get-tuple-element.19) | copy-start | bytes 9437188

commit v3 on v2

--- a/solution.py
+++ b/solution.py
@@ -275,87 +275,114 @@
     out.wait()
 
 
-def attn_kernel(chips, scale, q, do, kv, md, q_off, o_ref, dq_ref, dkv, s_scr, p_scr, ds_scr, acc_t, k_t, v_t, row_scr, m_ref, l_ref):
+def attn_kernel(chips, scale, q, do, kv, md, q_off, o_ref, dq_ref, dkv, s_scr, p_scr, acc_t, row_scr, m_ref, l_ref):
     pieces = 2 * chips
     tok = kv.shape[1] // 2 - 8
     head = kv.shape[2]
     lanes_all = q.shape[1]
     group = lanes_all // tok
     lw = 256
-    n_lc = lanes_all // lw
+    lanes = [slice(a, a + lw) for a in range(0, lanes_all, lw)]
     chip = lax.axis_index('cp') // 2
     dkv[...] = jnp.zeros_like(dkv)
-
-    def prep(j, tot):
-        v_t[j] = kv[j, tok:2 * tok].astype(F32).T.astype(BF16)
-        k_t[j] = kv[j, 0:tok].astype(F32).T.astype(BF16)
-        return tot + kv[j, 2 * tok:2 * tok + 16].astype(F32)
-
-    tot = lax.fori_loop(0, pieces, prep, jnp.zeros((16, head), F32))[0:1]
-
-    for pc in range(2):
-        place = chip if pc == 0 else pieces - 1 - chip
+    tot = lax.fori_loop(0, pieces, lambda j, a: a + kv[j, 2 * tok:2 * tok + 16].astype(F32), jnp.zeros((16, head), F32))[0:1]
+
+    @pl.loop(0, 2)
+    def _(pc):
+        place = jnp.where(pc == 0, chip, pieces - 1 - chip)
         doc_q = md[pc].astype(F32)[0:1]
         start = jnp.zeros((1, lanes_all), F32)
         for v in range(1, DOC_VALUES):
             start = jnp.where(doc_q == float(v), tot[:, v:v + 1], start)
         first = jnp.min(start).astype(jnp.int32) // tok
         pos = q_off[...] + (place * tok).astype(F32)
+        n_pair = (place - first + 2) // 2
         m_ref[...] = jnp.full_like(m_ref, NEG_BIG)
         l_ref[...] = jnp.zeros_like(l_ref)
 
-        @pl.loop(first, place + 1)
-        def _(kb):
-            keys = kv[kb, 0:tok]
-            u = (lax.broadcasted_iota(jnp.int32, (tok, lw), 0) + kb * tok).astype(F32)
-            for lc in range(n_lc):
-                ln = slice(lc * lw, (lc + 1) * lw)
+        def rows_of(t, base):
+            kb = place - 2 * t
+            return jnp.concatenate([kv[jnp.maximum(kb - 1, 0), base:base + tok], kv[kb, base:base + tok]], axis=0)
+
+        def add_rows(t, base, val):
+            kb = place - 2 * t
+            dkv[kb, base:base + tok] += val[tok:]
+            dkv[jnp.maximum(kb - 1, 0), base:base + tok] += val[:tok]
+
+        def score(t, masked):
+            keys = rows_of(t, 0)
+            u = (lax.broadcasted_iota(jnp.int32, (2 * tok, lw), 0) + (place - 2 * t - 1) * tok).astype(F32)
+            scales = []
+            for ln in lanes:
                 s = dot(keys, q[pc, ln], NT) * (scale * LOG2E)
-                s = jnp.where((u >= start[:, ln]) & (u <= pos[:, ln]), s, NEG_BIG)
-                s_scr[kb, :, ln] = s
+                if masked:
+                    s = jnp.where((u >= start[:, ln]) & (u <= pos[:, ln]), s, NEG_BIG)
+                s_scr[t, :, ln] = s
                 m_old = m_ref[:, ln]
                 m_new = jnp.maximum(m_old, jnp.max(s, axis=0, keepdims=True))
-                l_ref[:, ln] = l_ref[:, ln] * jnp.exp2(m_old - m_new) + jnp.sum(jnp.exp2(s - m_new), axis=0, keepdims=True)
                 m_ref[:, ln] = m_new
+                scales.append((m_new, jnp.exp2(m_old - m_new)))
+            for ln, (m_new, shrink) in zip(lanes, scales):
+                l_ref[:, ln] = l_ref[:, ln] * shrink + jnp.sum(jnp.exp2(s_scr[t, :, ln] - m_new), axis=0, keepdims=True)
+
+        last_start = (jnp.max(start).astype(jnp.int32) + tok - 1) // tok
+        n_full = jnp.maximum((place - last_start - 1) // 2, 0)
+
+        @pl.loop(0, n_pair)
+        def _(t):
+            inside = (t >= 1) & (t <= n_full)
+
+            @pl.when(inside)
+            def _():
+                score(t, False)
+
+            @pl.when(jnp.logical_not(inside))
+            def _():
+                score(t, True)
 
         log_norm = m_ref[...] + jnp.log2(l_ref[...])
         acc_t[...] = jnp.zeros_like(acc_t)
 
-        @pl.loop(first, place + 1)
-        def _(kb):
-            for lc in range(n_lc):
-                ln = slice(lc * lw, (lc + 1) * lw)
-                p = jnp.exp2(s_scr[kb, :, ln] - log_norm[:, ln]).astype(BF16)
-                p_scr[kb, :, ln] = p
-                acc_t[:, ln] += dot(v_t[kb], p)
-            dkv[kb, tok:2 * tok] += dot(p_scr[kb], do[pc])
-
-        for lc in range(n_lc):
-            ln = slice(lc * lw, (lc + 1) * lw)
+        @pl.loop(0, n_pair)
+        def _(t):
+            v_t = rows_of(t, tok).astype(F32).T.astype(BF16)
+            dv = jnp.zeros((2 * tok, head), F32)
+            for ln in lanes:
+                p = jnp.exp2(s_scr[t, :, ln] - log_norm[:, ln]).astype(BF16)
+                p_scr[t, :, ln] = p
+                acc_t[:, ln] += dot(v_t, p)
+                dv = dv + dot(p, do[pc, ln])
+            add_rows(t, tok, dv)
+
+        for ln in lanes:
             o_bf = acc_t[:, ln].astype(BF16).astype(F32)
             do_t = do[pc, ln].astype(F32).T
             l_ref[:, ln] = jnp.sum(do_t * o_bf, axis=0, keepdims=True)
             row_scr[ln, :] = o_bf.T.astype(BF16)
+        out_rows = pl.ds(pl.multiple_of(pc * tok, tok), tok)
         for g in range(group):
-            o_ref[pc * tok:(pc + 1) * tok, g * head:(g + 1) * head] = row_scr[g * tok:(g + 1) * tok, :]
+            o_ref[out_rows, g * head:(g + 1) * head] = row_scr[g * tok:(g + 1) * tok, :]
         acc_t[...] = jnp.zeros_like(acc_t)
 
-        @pl.loop(first, place + 1)
-        def _(kb):
-            vals = kv[kb, tok:2 * tok]
-            for lc in range(n_lc):
-                ln = slice(lc * lw, (lc + 1) * lw)
-                dp = dot(vals, do[pc, ln], NT)
-                ds = (p_scr[kb, :, ln].astype(F32) * (dp - l_ref[:, ln])).astype(BF16)
-                ds_scr[:, ln] = ds
-                acc_t[:, ln] += dot(k_t[kb], ds)
-            dkv[kb, 0:tok] += dot(ds_scr[...], q[pc]) * scale
-
-        for lc in range(n_lc):
-            ln = slice(lc * lw, (lc + 1) * lw)
+        @pl.loop(0, n_pair)
+        def _(t):
+            vals = rows_of(t, tok)
+            k_t = rows_of(t, 0).astype(F32).T.astype(BF16)
+            dk = jnp.zeros((2 * tok, head), F32)
+            nxt = dot(vals, do[pc, lanes[0]], NT)
+            for i, ln in enumerate(lanes):
+                dp = nxt
+                if i + 1 < len(lanes):
+                    nxt = dot(vals, do[pc, lanes[i + 1]], NT)
+                ds = (p_scr[t, :, ln].astype(F32) * (dp - l_ref[:, ln])).astype(BF16)
+                acc_t[:, ln] += dot(k_t, ds)
+                dk = dk + dot(ds, q[pc, ln])
+            add_rows(t, 0, dk * scale)
+
+        for ln in lanes:
             row_scr[ln, :] = (acc_t[:, ln] * scale).T.astype(BF16)
         for g in range(group):
-            dq_ref[pc * tok:(pc + 1) * tok, g * head:(g + 1) * head] = row_scr[g * tok:(g + 1) * tok, :]
+            dq_ref[out_rows, g * head:(g + 1) * head] = row_scr[g * tok:(g + 1) * tok, :]
 
 
 def out_kernel(chips, o, dq, dkv, wo, wq, wk, wv, y, dx,
@@ -500,20 +527,21 @@
     @pl.loop(0, n_x // 2)
     def _(h):
         x_step(2 * h, wr.at[0], wr.at[1])
-        event(3 + h)
+        event(3 + 2 * h)
         x_step(2 * h + 1, wr.at[1], wr.at[0])
+        event(4 + 2 * h)
 
     for c in wk_copies:
         c.wait()
     n_e = 2 * steps
-    first_e = 3 + n_x // 2
+    first_e = 3 + n_x
 
     @pl.loop(first_e, n_e)
     def _(e):
-        @pl.when(e < first_e + 4)
+        @pl.when(e < first_e + 2)
         def _():
             j = e - first_e
-            rows_b = d_half // 4
+            rows_b = d_half // 2
             piece = kc // 2
             for k in range(2):
                 for m in range(rows_b // piece):
@@ -625,8 +653,7 @@
             in_specs=[vmem_spec] * 5,
             out_specs=(vmem_spec,) * 3,
             scratch_shapes=[
-                pltpu.VMEM((pieces, tok, lanes), F32), pltpu.VMEM((pieces, tok, lanes), BF16), pltpu.VMEM((tok, lanes), BF16),
-                pltpu.VMEM((head, lanes), F32), pltpu.VMEM((pieces, head, tok), BF16), pltpu.VMEM((pieces, head, tok), BF16),
+                pltpu.VMEM((chips, rows2, lanes), F32), pltpu.VMEM((chips, rows2, lanes), BF16), pltpu.VMEM((head, lanes), F32),
                 pltpu.VMEM((lanes, head), BF16), pltpu.VMEM((1, lanes), F32), pltpu.VMEM((1, lanes), F32),
             ],
             compiler_params=pltpu.CompilerParams(vmem_limit_bytes=60 << 20),

time: 136 us -> 123 us (0.904)
  the two profiles are of different devices: /device:TPU:29 before, /device:TPU:23 now
where the time goes in v3:
time: 123 us; the launch traced here: 124 us
  Pallas kernels  115 us (93%)
  local copies, waits for them, and re-layouts  7.86 us (6%)
    pallas_call x1, Pallas kernels, local_layer(): pl.pallas_call(functools.partial(out_kernel, chips), name='out', out_shap...  58.7 us
    pallas_call x1, Pallas kernels, local_layer(): pl.pallas_call(functools.partial(proj_kernel, chips), name='proj', out_sh...  41.2 us
    pallas_call x1, Pallas kernels, local_layer(): pl.pallas_call(functools.partial(attn_kernel, chips, scale), name='attn',...  15.2 us
    unnamed x4, local copies, waits for them, and re-layouts  5.68 us

profile of v3, /device:TPU:23, one launch (start us, length us, event | category | flops | bytes accessed | tf_op | source)
XLA Modules:
  0.0 123.8 jit_solution(5572787812487121357)
XLA Ops:
  0.6 0.1 pad_add_fusion
  0.7 0.8 concatenate.19
  1.5 0.1 convert_reduce_fusion
  1.6 0.1 fusion
  1.7 0.1 concatenate.21
  1.8 0.7 broadcast_in_dim_tile.3.q_off
  2.5 0.7 broadcast_in_dim.7.meta
  3.1 41.2 %proj.1 = (bf16[2,1536,128]{2,1,0:T(8,128)(2,1)}, bf16[2,1536,128]{2,1,0:T(8,128)(2,1)}, bf16[16,400,128]{2,1,0:T(8,128)(2,1)}, bf16[2,16,1536]{2,1,0:T(8,128)(2,1)}) custom-call(bf16[192,8192]{1,0:T(8,128)(2,1)} %x.1, bf16[192,8192]{1,0:T(8,128)(2,1)} %dy.1, bf16[2,16,1664]{2,1,0:T(8,128)(2,1)} %broadcast_in_dim.7.meta, bf16[8192,2,8,128]{3,2,1,0:T(8,128)(2,1)} %bitcast.6, ...), custom_call_target="tpu_custom_call" | custom-call | tf_op jit(solution)/shard_map/proj/pallas_call | solution.py:627
  44.3 15.2 %attn.1 = (bf16[384,1024]{1,0:T(8,128)(2,1)}, bf16[384,1024]{1,0:T(8,128)(2,1)}, f32[16,384,128]{2,1,0:T(8,128)}) custom-call(bf16[2,1536,128]{2,1,0:T(8,128)(2,1)} %get-tuple-element.9.q, bf16[2,1536,128]{2,1,0:T(8,128)(2,1)} %get-tuple-element.10.do, bf16[16,400,128]{2,1,0:T(8,128)(2,1)} %get-tuple-element.11.kv, ...), custom_call_target="tpu_custom_call" | custom-call | tf_op jit(solution)/shard_map/attn/pallas_call | solution.py:648
  59.5 58.7 %out.1 = (bf16[192,8192]{1,0:T(8,128)(2,1)}, bf16[192,8192]{1,0:T(8,128)(2,1)}) custom-call(bf16[384,1024]{1,0:T(8,128)(2,1)} %get-tuple-element.13.o, bf16[384,1024]{1,0:T(8,128)(2,1)} %get-tuple-element.14.dq, f32[16,384,128]{2,1,0:T(8,128)} %get-tuple-element.15.dkv, bf16[2048,8192]{1,0:T(8,128)(2,1)} %bitcast.8, bf16[8192,16,128]{2,1,0:T(8,128)(2,1)} %wq.1, ...), custom_call_target="tpu_custom_call" | custom-call | tf_op jit(solution)/shard_map/out/pallas_call | solution.py:664
  118.1 0.0 copy-start
  118.2 4.0 %copy.11 = bf16[192,8192]{1,0:T(8,128)(2,1)} copy(bf16[192,8192]{1,0:T(8,128)(2,1)} %get-tuple-element.18) | data formatting | bytes 6291456
  122.2 0.0 copy-done
  122.2 1.7 %copy.12 = bf16[192,8192]{1,0:T(8,128)(2,1)} copy(bf16[192,8192]{1,0:T(8,128)(2,1)S(1)} %copy-done) | data formatting | bytes 6291456
  (5 shorter events, 0.0 us)
Async XLA Ops:
  118.1 4.0 %copy-start = (bf16[192,8192]{1,0:T(8,128)(2,1)S(1)}, bf16[192,8192]{1,0:T(8,128)(2,1)}, u32[]{:S(2)}) copy-start(bf16[192,8192]{1,0:T(8,128)(2,1)} %get-tuple-element.19) | copy-start | bytes 9437188

commit v4 on v3

--- a/solution.py
+++ b/solution.py
@@ -62,8 +62,8 @@
 
 
 def proj_kernel(chips, x, dy, meta, wq, wk, wv, wo, q_o, do_o, kv_o, md_o,
-                xb, dyb, mb, kvb, wkb, wvb, wqb, wob, wr, order, pick, wkv, acc, kvacc,
-                loc, wksem, wqsem, wosem, xs, xr, ys, yr, ms, mr, gs, gr, osem):
+                xb, dyb, mb, kvb, wkb, wvb, wqb, wob, wr, order, pick, wkv, acc, kvacc, kvx,
+                loc, wksem, wqsem, wosem, xs, xr, ys, yr, ms, mr, ks, kr, gs, gr, osem):
     half = x.shape[0] // 2
     d_model = x.shape[1]
     tok = 2 * half
@@ -112,61 +112,52 @@
     for s in range(wqb.shape[0]):
         wq_copy(s, s).start()
     entry_barrier((partner, up, down))
-    for c in x_rem:
+    m_rem.start()
+    for c in x_rem[:n_ch]:
         c.start()
-    m_rem.start()
-    for c in y_rem:
-        c.start()
-    for c in y_loc:
-        c.start()
-    for s in range(wob.shape[0]):
-        wo_copy(s, s).start()
-
+
+    n_sub = TILE // 2
     r = lax.broadcasted_iota(jnp.int32, pick.shape, 0)
-    pick[...] = jnp.where(lax.broadcasted_iota(jnp.int32, pick.shape, 1) == 2 * r + core, 1.0, 0.0).astype(BF16)
+    t = r & (n_sub - 1)
+    pick[...] = jnp.where(lax.broadcasted_iota(jnp.int32, pick.shape, 1) == 2 * t + jnp.where(r >= n_sub, 1, 0), 1.0, 0.0).astype(BF16)
     order[...] = sort_matrix()
-    n_sub = TILE // 2
     for ch in range(n_ch):
         for c in wk_copies[ch]:
             c.wait()
-        for j in range(ch * cw // n_sub, (ch + 1) * cw // n_sub, 2):
-            side = [buf[t * 2 * n_sub:(t + 1) * 2 * n_sub, :] for t in (j, j + 1) for buf in (wkb, wvb)]
-            rows = dot(pick[...], jnp.concatenate(side, axis=1)).astype(BF16)
-            wkv[j * n_sub:(j + 1) * n_sub, :] = rows[:, :2 * head]
-            wkv[(j + 1) * n_sub:(j + 2) * n_sub, :] = rows[:, 2 * head:]
-    quarters = 2
-    qs = qd // quarters
-
-    def split_part(slot, dst, k):
-        split_heads(order[...], wqb.at[slot, k * qs:(k + 1) * qs], dst.at[k * qs:(k + 1) * qs], qs, group, head)
-
-    wq_copy(0, 0).wait()
-    for k in range(quarters):
-        split_part(0, wr.at[0], k)
-    wq_copy(wqb.shape[0], 0).start()
-    for ch in range(n_ch):
+        for j in range(cw // n_sub):
+            src = slice((ch * cw + j * n_sub) * 2, (ch * cw + (j + 1) * n_sub) * 2)
+            rows = dot(pick[...], jnp.concatenate([wkb[src, :], wvb[src, :]], axis=1)).astype(BF16)
+            for h in range(2):
+                wkv[j * n_sub:(j + 1) * n_sub, h * 2 * head:(h + 1) * 2 * head] = rows[h * n_sub:(h + 1) * n_sub]
         for c in (x_loc[2 * ch], x_loc[2 * ch + 1]):
             c.wait()
-        for c in (x_rem[2 * ch], x_rem[2 * ch + 1]):
-            c.wait_recv()
-        hc = cw // 2
-        for k in range(2):
-            part_sum = dot(xb[:, ch * cw + k * hc:ch * cw + (k + 1) * hc], wkv[ch * cw + k * hc:ch * cw + (k + 1) * hc])
-            if ch == 0:
-                kvacc[k] = part_sum
-            else:
-                kvacc[k] += part_sum
+        part_sum = dot(jnp.concatenate([xb[pl.ds(row_off[pc], half), ch * cw:(ch + 1) * cw] for pc in range(2)], axis=0), wkv[...])
+        if ch == 0:
+            kvacc[...] = part_sum
+        else:
+            kvacc[...] += part_sum
+    both_heads = [kvacc[:, h * 2 * head:(h + 1) * 2 * head] for h in range(2)]
+    kvx[0] = jnp.where(core == 0, both_heads[1], both_heads[0]).astype(BF16)
+    kvx[1] = jnp.where(core == 0, both_heads[0], both_heads[1]).astype(BF16)
+    k_rem = remote(kvx.at[0], kvx.at[2], ks, kr, partner)
+    k_rem.start()
+    for c in x_rem[n_ch:]:
+        c.start()
     m_loc.wait()
     m_rem.wait_recv()
     lo, hi = chip, pieces - 1 - chip
     width = md_o.shape[2]
+    own_off = (pl.multiple_of(half * core, half), pl.multiple_of(half - half * core, half))
     for pc, idx in ((0, lo), (1, hi)):
         both = (mb[0, pc].astype(F32) + mb[1, pc].astype(F32)).astype(BF16)
         md_o[pc] = both[:, :width]
         kvb[idx, 2 * tok:2 * tok + 16] = both[:, width:]
-        kv_sum = (kvacc[0, pc * tok:(pc + 1) * tok, :] + kvacc[1, pc * tok:(pc + 1) * tok, :]).astype(BF16)
-        kvb[idx, 0:tok] = kv_sum[:, 0:head]
-        kvb[idx, tok:2 * tok] = kv_sum[:, head:]
+        for k in range(2):
+            kvb[idx, pl.ds(k * tok + own_off[pc], half)] = kvx[1, pc * half:(pc + 1) * half, k * head:(k + 1) * head]
+    k_rem.wait_recv()
+    for pc, idx in ((0, lo), (1, hi)):
+        for k in range(2):
+            kvb[idx, pl.ds(k * tok + own_off[1 - pc], half)] = kvx[2, pc * half:(pc + 1) * half, k * head:(k + 1) * head]
 
     last = chips // 2 - 1
 
@@ -192,6 +183,23 @@
     for d, pc in moves[0]:
         hop(d, 0, pc).start()
 
+    for c in y_rem:
+        c.start()
+    for c in y_loc:
+        c.start()
+    for k in range(wob.shape[0]):
+        wo_copy(k, k).start()
+    quarters = 2
+    qs = qd // quarters
+
+    def split_part(slot, dst, k):
+        split_heads(order[...], wqb.at[slot, k * qs:(k + 1) * qs], dst.at[k * qs:(k + 1) * qs], qs, group, head)
+
+    wq_copy(0, 0).wait()
+    for k in range(quarters):
+        split_part(0, wr.at[0], k)
+    wq_copy(wqb.shape[0], 0).start()
+
     acc[...] = jnp.zeros_like(acc)
     n_slot = wqb.shape[0]
     nw = group * head // quarters
@@ -213,22 +221,21 @@
         def _():
             wq_copy(i + 1 + n_slot, slot).start()
 
+    plan = {1: (1, 0), 3: (1, 1), 4: (2, 0), 6: (2, 1), 7: (3, 0)}
+
     @pl.loop(0, n_q // 2)
     def _(h):
-        q_step(2 * h, wr.at[0], wr.at[1])
-        q_step(2 * h + 1, wr.at[1], wr.at[0])
-
-        @pl.when(h == 1)
-        def _():
-            advance(1, 0)
-
-        @pl.when(h == 2)
-        def _():
-            advance(1, 1)
-
-        @pl.when(h == 3)
-        def _():
-            advance(2, 0)
+        cols = pl.ds(pl.multiple_of(h * 2 * qd, 2 * qd), 2 * qd)
+        for pc in range(2):
+            rows = xb.at[pl.ds(row_off[pc], half), cols]
+            remote(rows, rows, xs.at[pc, h], xr.at[pc, h], partner).wait_recv()
+        for k in range(2):
+            q_step(2 * h + k, wr.at[k], wr.at[1 - k])
+            for at, step in plan.items():
+                if at % 2 == k:
+                    @pl.when(h == at // 2)
+                    def _():
+                        advance(*step)
 
     for g in range(group):
         for pc in range(2):
@@ -258,16 +265,12 @@
                 for pc in range(2):
                     do_o[pc, (n * wide + g) * tok:(n * wide + g + 1) * tok, :] = acc[pc * tok:(pc + 1) * tok, g * head:(g + 1) * head].astype(BF16)
         if u == 0:
-            advance(2, 1)
-        elif u == 1:
-            advance(3, 0)
-        elif u == 2:
             advance(3, 1)
     for t in range(4, last + 2):
         advance(t)
     out = pltpu.make_async_copy(kvb, kv_o, osem.at[0])
     out.start()
-    for c in x_rem + y_rem + [m_rem]:
+    for c in x_rem + y_rem + [m_rem, k_rem]:
         c.wait_send()
     for t in range(last + 1):
         for d, pc in moves[t]:
@@ -275,7 +278,7 @@
     out.wait()
 
 
-def attn_kernel(chips, scale, q, do, kv, md, q_off, o_ref, dq_ref, dkv, s_scr, p_scr, acc_t, row_scr, m_ref, l_ref):
+def attn_kernel(chips, scale, q, do, kv, md, o_ref, dq_ref, dkv, s_scr, p_scr, acc_t, row_scr, m_ref, l_ref):
     pieces = 2 * chips
     tok = kv.shape[1] // 2 - 8
     head = kv.shape[2]
@@ -285,6 +288,10 @@
     lanes = [slice(a, a + lw) for a in range(0, lanes_all, lw)]
     chip = lax.axis_index('cp') // 2
     dkv[...] = jnp.zeros_like(dkv)
+    lane = lax.broadcasted_iota(jnp.int32, (1, lanes_all), 1)
+    for g in range(1, group):
+        lane = jnp.where(lane >= tok, lane - tok, lane)
+    q_off = lane.astype(F32)
     tot = lax.fori_loop(0, pieces, lambda j, a: a + kv[j, 2 * tok:2 * tok + 16].astype(F32), jnp.zeros((16, head), F32))[0:1]
 
     @pl.loop(0, 2)
@@ -295,7 +302,7 @@
         for v in range(1, DOC_VALUES):
             start = jnp.where(doc_q == float(v), tot[:, v:v + 1], start)
         first = jnp.min(start).astype(jnp.int32) // tok
-        pos = q_off[...] + (place * tok).astype(F32)
+        pos = q_off + (place * tok).astype(F32)
         n_pair = (place - first + 2) // 2
         m_ref[...] = jnp.full_like(m_ref, NEG_BIG)
         l_ref[...] = jnp.zeros_like(l_ref)
@@ -612,7 +619,6 @@
         counts = jnp.sum((docs[:, :, None] < jnp.arange(head)[None, None, :]).astype(F32), axis=1)
         meta = jnp.concatenate([ids, counts], axis=1).astype(BF16)
         meta = jnp.broadcast_to(meta[:, None, :], (2, 16, lanes + head))
-        q_off = jnp.tile(lane.astype(F32), (group,))[None, :]
 
         wq4 = w_q.reshape(d_model, kv_heads, group, head)
         wk2 = w_k.reshape(d_model * kv_heads, head)
@@ -636,10 +642,10 @@
                 pltpu.VMEM((pieces, kv_rows, head), BF16),
                 pltpu.VMEM((2 * d_model, head), BF16), pltpu.VMEM((2 * d_model, head), BF16),
                 pltpu.VMEM((3, qd, group, head), BF16), pltpu.VMEM((2, 4 * head, d_model // 2), BF16),
-                pltpu.VMEM((2, qd, group * head), BF16), pltpu.VMEM((TILE, TILE), BF16), pltpu.VMEM((TILE // 2, TILE), BF16), pltpu.VMEM((d_model, 2 * head), BF16),
-                pltpu.VMEM((rows2, group * head), F32), pltpu.VMEM((2, rows2, 2 * head), F32),
+                pltpu.VMEM((2, qd, group * head), BF16), pltpu.VMEM((TILE, TILE), BF16), pltpu.VMEM((TILE, TILE), BF16), pltpu.VMEM((cw, 4 * head), BF16),
+                pltpu.VMEM((rows2, group * head), F32), pltpu.VMEM((tok, 4 * head), F32), pltpu.VMEM((3, tok, 2 * head), BF16),
                 dma((2, 2, n_ch)), dma((2, n_ch)), dma((3,)), dma((2,)),
-                dma((2, n_ch)), dma((2, n_ch)), dma((2, n_ch)), dma((2, n_ch)), dma, dma,
+                dma((2, n_ch)), dma((2, n_ch)), dma((2, n_ch)), dma((2, n_ch)), dma, dma, dma, dma,
                 dma((2, hops, 2)), dma((2, hops, 2)), dma((1,)),
             ],
             compiler_params=pltpu.CompilerParams(collective_id=0, has_side_effects=True, vmem_limit_bytes=60 << 20),
@@ -650,14 +656,14 @@
             name='attn',
             out_shape=(jax.ShapeDtypeStruct((rows2, group * head), BF16), jax.ShapeDtypeStruct((rows2, group * head), BF16),
                        jax.ShapeDtypeStruct((pieces, 2 * tok, head), F32)),
-            in_specs=[vmem_spec] * 5,
+            in_specs=[vmem_spec] * 4,
             out_specs=(vmem_spec,) * 3,
             scratch_shapes=[
                 pltpu.VMEM((chips, rows2, lanes), F32), pltpu.VMEM((chips, rows2, lanes), BF16), pltpu.VMEM((head, lanes), F32),
                 pltpu.VMEM((lanes, head), BF16), pltpu.VMEM((1, lanes), F32), pltpu.VMEM((1, lanes), F32),
             ],
             compiler_params=pltpu.CompilerParams(vmem_limit_bytes=60 << 20),
-        )(q, do, kv, md, q_off)
+        )(q, do, kv, md)
 
         steps = chips - 1
         bw = d_half // 8

time: 123 us -> 119 us (0.967)
  the two profiles are of different devices: /device:TPU:23 before, /device:TPU:21 now
where the time goes in v4:
time: 119 us; the launch traced here: 117 us
  Pallas kernels  109 us (92%)
  local copies, waits for them, and re-layouts  7.19 us (6%)
    pallas_call x1, Pallas kernels, local_layer(): pl.pallas_call(functools.partial(out_kernel, chips), name='out', out_shap...  55.5 us
    pallas_call x1, Pallas kernels, local_layer(): pl.pallas_call(functools.partial(proj_kernel, chips), name='proj', out_sh...  41.7 us
    pallas_call x1, Pallas kernels, local_layer(): pl.pallas_call(functools.partial(attn_kernel, chips, scale), name='attn',...  12.2 us
    unnamed x4, local copies, waits for them, and re-layouts  5.68 us

profile of v4, /device:TPU:21, one launch (start us, length us, event | category | flops | bytes accessed | tf_op | source)
XLA Modules:
  0.0 117.5 jit_solution(17741548522451288670)
XLA Ops:
  0.6 0.1 pad_add_fusion
  0.7 0.8 concatenate.19
  1.5 0.1 convert_reduce_fusion
  1.6 0.1 fusion
  1.7 0.1 concatenate.21
  1.8 0.7 broadcast_in_dim.7.meta
  2.4 41.7 %proj.1 = (bf16[2,1536,128]{2,1,0:T(8,128)(2,1)}, bf16[2,1536,128]{2,1,0:T(8,128)(2,1)}, bf16[16,400,128]{2,1,0:T(8,128)(2,1)}, bf16[2,16,1536]{2,1,0:T(8,128)(2,1)}) custom-call(bf16[192,8192]{1,0:T(8,128)(2,1)} %x.1, bf16[192,8192]{1,0:T(8,128)(2,1)} %dy.1, bf16[2,16,1664]{2,1,0:T(8,128)(2,1)} %broadcast_in_dim.7.meta, bf16[8192,2,8,128]{3,2,1,0:T(8,128)(2,1)} %bitcast.6, ...), custom_call_target="tpu_custom_call" | custom-call | tf_op jit(solution)/shard_map/proj/pallas_call | solution.py:633
  44.1 12.2 %attn.1 = (bf16[384,1024]{1,0:T(8,128)(2,1)}, bf16[384,1024]{1,0:T(8,128)(2,1)}, f32[16,384,128]{2,1,0:T(8,128)}) custom-call(bf16[2,1536,128]{2,1,0:T(8,128)(2,1)} %get-tuple-element.9.q, bf16[2,1536,128]{2,1,0:T(8,128)(2,1)} %get-tuple-element.10.do, bf16[16,400,128]{2,1,0:T(8,128)(2,1)} %get-tuple-element.11.kv, bf16[2,16,1536]{2,1,0:T(8,128)(2,1)} %get-tuple-element.12.md), custom_call_target="tpu_custom_call" | custom-call | tf_op jit(solution)/shard_map/attn/pallas_call | solution.py:654
  56.3 55.5 %out.1 = (bf16[192,8192]{1,0:T(8,128)(2,1)}, bf16[192,8192]{1,0:T(8,128)(2,1)}) custom-call(bf16[384,1024]{1,0:T(8,128)(2,1)} %get-tuple-element.13.o, bf16[384,1024]{1,0:T(8,128)(2,1)} %get-tuple-element.14.dq, f32[16,384,128]{2,1,0:T(8,128)} %get-tuple-element.15.dkv, bf16[2048,8192]{1,0:T(8,128)(2,1)} %bitcast.8, bf16[8192,16,128]{2,1,0:T(8,128)(2,1)} %wq.1, ...), custom_call_target="tpu_custom_call" | custom-call | tf_op jit(solution)/shard_map/out/pallas_call | solution.py:670
  111.8 0.0 copy-start
  111.8 4.0 %copy.11 = bf16[192,8192]{1,0:T(8,128)(2,1)} copy(bf16[192,8192]{1,0:T(8,128)(2,1)} %get-tuple-element.18) | data formatting | bytes 6291456
  115.8 0.0 copy-done
  115.8 1.7 %copy.12 = bf16[192,8192]{1,0:T(8,128)(2,1)} copy(bf16[192,8192]{1,0:T(8,128)(2,1)S(1)} %copy-done) | data formatting | bytes 6291456
  (3 shorter events, 0.0 us)
Async XLA Ops:
  111.8 4.0 %copy-start = (bf16[192,8192]{1,0:T(8,128)(2,1)S(1)}, bf16[192,8192]{1,0:T(8,128)(2,1)}, u32[]{:S(2)}) copy-start(bf16[192,8192]{1,0:T(8,128)(2,1)} %get-tuple-element.19) | copy-start | bytes 9437188

commit v5 on v4

--- a/solution.py
+++ b/solution.py
@@ -143,6 +143,17 @@
     k_rem.start()
     for c in x_rem[n_ch:]:
         c.start()
+    quarters = 2
+    qs = qd // quarters
+
+    def split_part(slot, dst, k):
+        split_heads(order[...], wqb.at[slot, k * qs:(k + 1) * qs], dst.at[k * qs:(k + 1) * qs], qs, group, head)
+
+    wq_copy(0, 0).wait()
+    for k in range(quarters):
+        split_part(0, wr.at[0], k)
+    wq_copy(wqb.shape[0], 0).start()
+
     m_loc.wait()
     m_rem.wait_recv()
     lo, hi = chip, pieces - 1 - chip
@@ -189,16 +200,6 @@
         c.start()
     for k in range(wob.shape[0]):
         wo_copy(k, k).start()
-    quarters = 2
-    qs = qd // quarters
-
-    def split_part(slot, dst, k):
-        split_heads(order[...], wqb.at[slot, k * qs:(k + 1) * qs], dst.at[k * qs:(k + 1) * qs], qs, group, head)
-
-    wq_copy(0, 0).wait()
-    for k in range(quarters):
-        split_part(0, wr.at[0], k)
-    wq_copy(wqb.shape[0], 0).start()
 
     acc[...] = jnp.zeros_like(acc)
     n_slot = wqb.shape[0]
@@ -455,10 +456,10 @@
         return remote(src, ring.at[direction, s, kvp], rs.at[direction, s, kvp], rr.at[direction, s, kvp], up if direction == 0 else down)
 
     def event(e):
-        s, kvp = e // 2 + 1, lax.rem(e, 2)
+        s, kvp = e // 2 + 1, e % 2 if isinstance(e, int) else lax.rem(e, 2)
         for d in range(2):
             remote(ring.at[d, s - 1, kvp], ring.at[d, s - 1, kvp], rs.at[d, s - 1, kvp], rr.at[d, s - 1, kvp], up).wait_recv()
-            ring[d, s - 1, kvp] = ring[d, s - 1, kvp] + own[owner(d, s), part_rows(pl.multiple_of(kvp * tok, tok))]
+            ring[d, s - 1, kvp] = ring[d, s - 1, kvp] + own[owner(d, s), part_rows(kvp * tok if isinstance(e, int) else pl.multiple_of(kvp * tok, tok))]
 
         @pl.when(s < steps)
         def _():
@@ -477,8 +478,22 @@
             pltpu.make_async_copy(buf.at[pl.ds(mine[pc], half), bc], dst.at[pl.ds(half * pc, half), cols], lsem).start()
             remote(buf.at[pl.ds(theirs[pc], half), bc], dst.at[pl.ds(half * pc, half), cols], ssem, rsem, partner).start()
 
+    nq = wqb.shape[0]
+    quarters = 2
+    qs = qd // quarters
+    order[...] = sort_matrix()
+
+    def split_part(slot, dst, k):
+        split_heads(order[...], wqb.at[slot, k * qs:(k + 1) * qs], dst.at[k * qs:(k + 1) * qs], qs, n_head, head)
+
+    wq_copy(0, 0).wait()
+    for k in range(quarters):
+        split_part(0, wr.at[0], k)
+    wq_copy(nq, 0).start()
+
     l_o.wait()
     r_o.wait_recv()
+    event(0)
     ns = wob.shape[0]
 
     @pl.loop(0, n_y)
@@ -495,27 +510,14 @@
         def _():
             out_copies(yb, y, i - 1, bw, ysem, ys, yr)
 
-        @pl.when((i >= 3) & (lax.rem(i, 2) == 1))
-        def _():
-            event((i - 3) // 2)
+        @pl.when(lax.rem(i, 2) == 1)
+        def _():
+            event((i + 1) // 2)
 
     out_copies(yb, y, n_y - 1, bw, ysem, ys, yr)
 
     l_dq.wait()
     r_dq.wait_recv()
-    nq = wqb.shape[0]
-    quarters = 2
-    qs = qd // quarters
-    order[...] = sort_matrix()
-
-    def split_part(slot, dst, k):
-        split_heads(order[...], wqb.at[slot, k * qs:(k + 1) * qs], dst.at[k * qs:(k + 1) * qs], qs, n_head, head)
-
-    wq_copy(0, 0).wait()
-    for k in range(quarters):
-        split_part(0, wr.at[0], k)
-    wq_copy(nq, 0).start()
-
     def x_step(i, cur, nxt):
         slot = lax.rem(i + 1, nq)
 
@@ -534,29 +536,26 @@
     @pl.loop(0, n_x // 2)
     def _(h):
         x_step(2 * h, wr.at[0], wr.at[1])
-        event(3 + 2 * h)
+        event(5 + 2 * h)
         x_step(2 * h + 1, wr.at[1], wr.at[0])
-        event(4 + 2 * h)
+        event(6 + 2 * h)
 
     for c in wk_copies:
         c.wait()
     n_e = 2 * steps
-    first_e = 3 + n_x
-
-    @pl.loop(first_e, n_e)
-    def _(e):
-        @pl.when(e < first_e + 2)
-        def _():
-            j = e - first_e
-            rows_b = d_half // 2
-            piece = kc // 2
-            for k in range(2):
-                for m in range(rows_b // piece):
-                    r0 = pl.multiple_of(j * rows_b + m * piece, piece)
-                    scr[k * kc:(k + 1) * kc, :] = wkb[k, pl.ds(2 * r0, kc), :].astype(F32)
-                    for h in range(2):
-                        b2[pl.ds(r0, piece), (2 * k + h) * head:(2 * k + h + 1) * head] = scr[pl.ds(k * kc + h, piece, stride=2), :].astype(BF16)
-
+
+    @pl.loop(0, 2)
+    def _(j):
+        rows_b = d_half // 2
+        piece = kc // 2
+        for k in range(2):
+            for m in range(rows_b // piece):
+                r0 = pl.multiple_of(j * rows_b + m * piece, piece)
+                scr[k * kc:(k + 1) * kc, :] = wkb[k, pl.ds(2 * r0, kc), :].astype(F32)
+                for h in range(2):
+                    b2[pl.ds(r0, piece), (2 * k + h) * head:(2 * k + h + 1) * head] = scr[pl.ds(k * kc + h, piece, stride=2), :].astype(BF16)
+
+    for e in range(5 + n_x, n_e):
         event(e)
 
     for kvp in range(2):

time: 119 us -> 115 us (0.966)
  Pallas kernels: 109 us -> 106 us
    pallas_call x1, Pallas kernels: 41.7 us -> 39.6 us  [local_layer(): pl.pallas_call(functools.partial(proj_kernel, chips), name='proj', out_sh...]
where the time goes in v5:
time: 115 us; the launch traced here: 114 us
  Pallas kernels  106 us (92%)
  local copies, waits for them, and re-layouts  7.19 us (6%)
    pallas_call x1, Pallas kernels, local_layer(): pl.pallas_call(functools.partial(out_kernel, chips), name='out', out_shap...  54.4 us
    pallas_call x1, Pallas kernels, local_layer(): pl.pallas_call(functools.partial(proj_kernel, chips), name='proj', out_sh...  39.6 us
    pallas_call x1, Pallas kernels, local_layer(): pl.pallas_call(functools.partial(attn_kernel, chips, scale), name='attn',...  12.2 us
    unnamed x4, local copies, waits for them, and re-layouts  5.68 us

profile of v5, /device:TPU:21, one launch (start us, length us, event | category | flops | bytes accessed | tf_op | source)
XLA Modules:
  0.0 114.4 jit_solution(10613933197938362247)
XLA Ops:
  0.6 0.1 pad_add_fusion
  0.7 0.8 concatenate.19
  1.5 0.1 convert_reduce_fusion
  1.6 0.1 fusion
  1.7 0.1 concatenate.21
  1.8 0.7 broadcast_in_dim.7.meta
  2.4 39.6 %proj.1 = (bf16[2,1536,128]{2,1,0:T(8,128)(2,1)}, bf16[2,1536,128]{2,1,0:T(8,128)(2,1)}, bf16[16,400,128]{2,1,0:T(8,128)(2,1)}, bf16[2,16,1536]{2,1,0:T(8,128)(2,1)}) custom-call(bf16[192,8192]{1,0:T(8,128)(2,1)} %x.1, bf16[192,8192]{1,0:T(8,128)(2,1)} %dy.1, bf16[2,16,1664]{2,1,0:T(8,128)(2,1)} %broadcast_in_dim.7.meta, bf16[8192,2,8,128]{3,2,1,0:T(8,128)(2,1)} %bitcast.6, ...), custom_call_target="tpu_custom_call" | custom-call | tf_op jit(solution)/shard_map/proj/pallas_call | solution.py:632
  42.1 12.2 %attn.1 = (bf16[384,1024]{1,0:T(8,128)(2,1)}, bf16[384,1024]{1,0:T(8,128)(2,1)}, f32[16,384,128]{2,1,0:T(8,128)}) custom-call(bf16[2,1536,128]{2,1,0:T(8,128)(2,1)} %get-tuple-element.9.q, bf16[2,1536,128]{2,1,0:T(8,128)(2,1)} %get-tuple-element.10.do, bf16[16,400,128]{2,1,0:T(8,128)(2,1)} %get-tuple-element.11.kv, bf16[2,16,1536]{2,1,0:T(8,128)(2,1)} %get-tuple-element.12.md), custom_call_target="tpu_custom_call" | custom-call | tf_op jit(solution)/shard_map/attn/pallas_call | solution.py:653
  54.3 54.4 %out.1 = (bf16[192,8192]{1,0:T(8,128)(2,1)}, bf16[192,8192]{1,0:T(8,128)(2,1)}) custom-call(bf16[384,1024]{1,0:T(8,128)(2,1)} %get-tuple-element.13.o, bf16[384,1024]{1,0:T(8,128)(2,1)} %get-tuple-element.14.dq, f32[16,384,128]{2,1,0:T(8,128)} %get-tuple-element.15.dkv, bf16[2048,8192]{1,0:T(8,128)(2,1)} %bitcast.8, bf16[8192,16,128]{2,1,0:T(8,128)(2,1)} %wq.1, ...), custom_call_target="tpu_custom_call" | custom-call | tf_op jit(solution)/shard_map/out/pallas_call | solution.py:669
  108.7 0.0 copy-start
  108.7 4.0 %copy.11 = bf16[192,8192]{1,0:T(8,128)(2,1)} copy(bf16[192,8192]{1,0:T(8,128)(2,1)} %get-tuple-element.18) | data formatting | bytes 6291456
  112.7 0.0 copy-done
  112.7 1.7 %copy.12 = bf16[192,8192]{1,0:T(8,128)(2,1)} copy(bf16[192,8192]{1,0:T(8,128)(2,1)S(1)} %copy-done) | data formatting | bytes 6291456
  (3 shorter events, 0.0 us)
Async XLA Ops:
  108.7 4.0 %copy-start = (bf16[192,8192]{1,0:T(8,128)(2,1)S(1)}, bf16[192,8192]{1,0:T(8,128)(2,1)}, u32[]{:S(2)}) copy-start(bf16[192,8192]{1,0:T(8,128)(2,1)} %get-tuple-element.19) | copy-start | bytes 9437188
